TPU v7x, 128 devices: a whole 4x4x4 slice. The times are simulated.
128 devices in a mesh: emb: 32 (over z, x, core), seq: 4 (over y).
Axes of the slice: x: 4, y: 4, z: 4, core: 2. Of those that a mesh axis runs over, the one named last changes fastest.
Arguments:
- item_table: bfloat16 [131072, 512], P('emb'), may hold values from -6 to 6
- fetch_rows: int32 [32, 4, 32, 16], P('emb', 'seq'), may hold values from 0 to 4095
- event_slot: int32 [131072], P(('emb', 'seq')), may hold values from 0 to 511, as said below
- lengths: int32 [128, 8], P(('emb', 'seq')), may hold values from 1 to 512, 1024 in all within a row
- in_weight: bfloat16 [512, 2048], replicated, may hold values from -0.25 to 0.25
- out_weight: bfloat16 [512, 512], replicated, may hold values from -0.25 to 0.25
- out_grad: bfloat16 [131072, 512], P(('emb', 'seq')), may hold values from -6 to 6
Outputs:
- layer_out: bfloat16 [131072, 512], P(('emb', 'seq'))
- table_grad: float32 [131072, 512], P(('emb', 'seq'))
- in_weight_grad: float32 [512, 2048], replicated
- out_weight_grad: float32 [512, 512], replicated
Inputs may be any that keep to these rules, and one draw needn't show every extreme that they name: `event_slot`: within each buffer of 1024 events every slot 0 to 511 is named by at least one event.
All inputs are finite; a program needn't handle non-finite values.
Results may differ from a plain program's by a relative error of at most 0.02.
Values may be sent and summed in bfloat16 or wider, within the bound.
A program may use at most 192 MiB of HBM per device.

v0:
```python
import jax
import jax.numpy as jnp
from jax import lax
from jax.sharding import PartitionSpec as P

HEADS = 4
MOST = 512


EPS = 1e-05


def in_one_piece(arrays, axis, split_dim, concat_dim, along):
    both = jnp.concatenate(arrays, axis=along)
    out, at, done = (
        lax.all_to_all(both, axis, split_axis=split_dim, concat_axis=concat_dim, tiled=True),
        0,
        [],
    )
    for a in arrays:
        done.append(lax.slice_in_dim(out, at, at + a.shape[along], axis=along))
        at += a.shape[along]
    return tuple(done)


def in_one_piece_2(arrays, axis, dim, along):
    both = jnp.concatenate(arrays, axis=along)
    out, at, done = (lax.all_gather(both, axis, axis=dim, tiled=True), 0, [])
    for a in arrays:
        done.append(lax.slice_in_dim(out, at, at + a.shape[along], axis=along))
        at += a.shape[along]
    return tuple(done)


def normalize(rows_in):
    center = rows_in - jnp.mean(rows_in, axis=-1, keepdims=True)
    spread = jnp.mean(center * center, axis=-1, keepdims=True)
    return center * lax.rsqrt(spread + EPS)


def hstu_layer(events, in_weight, out_weight, lengths_row):
    rows_count, model_width = events.shape
    head_size = model_width // HEADS
    normed = normalize(events.astype(jnp.float32)).astype(jnp.bfloat16)
    hidden = jax.nn.silu(jnp.dot(normed, in_weight, preferred_element_type=jnp.float32))
    update_gate = hidden[:, :model_width]
    values = (
        hidden[:, model_width : 2 * model_width]
        .astype(jnp.bfloat16)
        .reshape(rows_count, HEADS, head_size)
    )
    queries = (
        hidden[:, 2 * model_width : 3 * model_width]
        .astype(jnp.bfloat16)
        .reshape(rows_count, HEADS, head_size)
    )
    key_rows = (
        hidden[:, 3 * model_width :].astype(jnp.bfloat16).reshape(rows_count, HEADS, head_size)
    )
    scores = jnp.einsum(
        "ihd,jhd->hij", queries, key_rows, preferred_element_type=jnp.float32
    ) * head_size ** (-0.5)
    places = jnp.arange(rows_count, dtype=jnp.int32)
    seq_ends = jnp.cumsum(lengths_row)
    segment = jnp.sum((places[:, None] >= seq_ends[None, :]).astype(jnp.int32), axis=1)
    allowed = (segment[:, None] == segment[None, :]) & (places[None, :] <= places[:, None])
    weights = jnp.where(allowed[None], jax.nn.silu(scores) / MOST, 0.0).astype(jnp.bfloat16)
    attended = jnp.einsum(
        "hij,jhd->ihd", weights, values, preferred_element_type=jnp.float32
    ).reshape(rows_count, model_width)
    gated_rows = (normalize(attended) * update_gate).astype(jnp.bfloat16)
    return (
        jnp.dot(gated_rows, out_weight, preferred_element_type=jnp.float32)
        + events.astype(jnp.float32)
    ).astype(jnp.bfloat16)


def on_device(item_table, fetch_rows, event_slot, lengths, in_weight, out_weight, out_grad):
    emb_count = lax.axis_size("emb")
    seq_count = lax.axis_size("seq")
    model_width = item_table.shape[1]
    shard_rows = item_table.shape[0]
    requests = fetch_rows.reshape(emb_count, -1)
    slot_count = requests.shape[0] * requests.shape[1]
    asked_rows = lax.all_to_all(requests, "emb", split_axis=0, concat_axis=0, tiled=True)
    found = item_table[asked_rows]
    fetched, asked_rows = (
        lax.all_to_all(found, "emb", split_axis=0, concat_axis=0, tiled=True),
        asked_rows,
    )
    slot_table = fetched.reshape(slot_count, model_width)
    events = slot_table[event_slot]
    lengths_row = lengths[0]

    def forward(rows_x, first, second):
        return hstu_layer(rows_x, first, second, lengths_row)

    layer_out, pullback = jax.vjp(forward, events, in_weight, out_weight)
    row_grad, first_grad, second_grad = pullback(out_grad)
    slot_grad = jax.ops.segment_sum(
        row_grad.astype(jnp.float32), event_slot, num_segments=slot_count
    )
    returned = lax.all_to_all(
        slot_grad.reshape(emb_count, -1, model_width).astype(jnp.bfloat16),
        "emb",
        split_axis=0,
        concat_axis=0,
        tiled=True,
    ).astype(jnp.float32)
    owner_sum = jax.ops.segment_sum(
        returned.reshape(-1, model_width), asked_rows.reshape(-1), num_segments=shard_rows
    )
    table_grad = lax.psum_scatter(
        owner_sum.astype(jnp.bfloat16), "seq", scatter_dimension=0, tiled=True
    ).astype(jnp.float32)
    members = emb_count * seq_count
    first_cut = first_grad.reshape(members, -1)
    second_cut = second_grad.reshape(members, -1)
    got_first, got_second = in_one_piece((first_cut, second_cut), ("emb", "seq"), 0, 0, 1)
    own_first = jnp.sum(got_first.astype(jnp.float32), axis=0, keepdims=True)
    own_second = jnp.sum(got_second.astype(jnp.float32), axis=0, keepdims=True)
    whole_first, whole_second = tuple(
        (
            part.astype(jnp.float32)
            for part in in_one_piece_2(
                (own_first.astype(jnp.bfloat16), own_second.astype(jnp.bfloat16)),
                ("emb", "seq"),
                0,
                1,
            )
        )
    )
    in_total = whole_first.reshape(first_grad.shape)
    out_total = whole_second.reshape(second_grad.shape)
    return (layer_out, table_grad, in_total, out_total)


def solution(mesh):
    placed = (
        P("emb", None),
        P("emb", "seq", None, None),
        P(("emb", "seq")),
        P(("emb", "seq"), None),
        P(),
        P(),
        P(("emb", "seq"), None),
    )
    return jax.shard_map(
        on_device,
        mesh=mesh,
        in_specs=placed,
        out_specs=(P(("emb", "seq"), None), P(("emb", "seq"), None), P(), P()),
        check_vma=False,
    )
```

profile of v0, /device:TPU:1, one launch (start us, length us, event | category | flops | bytes accessed | tf_op | source)
XLA Modules:
  0.0 339.9 jit_solution(18004084113317078172)
XLA Ops:
  8.9 16.2 %all_to_all.34 = s32[32,1,16]{2,1,0:T(1,128)S(1)} all-to-all(s32[32,1,16]{2,1,0:T(1,128)S(1)} %bitcast.89), channel_id=1, replica_groups=mesh['emb'=32,'seq'=4] {'emb'}, dimensions={0} | all-to-all | bytes 4096 | tf_op jit(solution)/shard_map/all_to_all | solution.py:85
  25.2 5.4 %gather_fusion = bf16[512,512]{1,0:T(8,128)(2,1)} fusion(bf16[4096,512]{1,0:T(8,128)(2,1)} %param.7, s32[1024]{0:T(1024)S(1)} %pad_clamp_fusion), kind=kCustom, calls=%fused_computation | custom fusion | bytes 1050624 | tf_op jit(solution)/shard_map/gather | solution.py:86
  30.6 4.2 %all-to-all-start.1 = ((bf16[32,16,512]{2,1,0:T(8,128)(2,1)}), bf16[32,16,512]{2,1,0:T(8,128)(2,1)S(1)}, u32[]{:S(2)}, u32[]{:S(2)}) async-start(bf16[32,16,512]{2,1,0:T(8,128)(2,1)} %bitcast.2), calls=%async_computation.1 | async-start | bytes 1048576 | tf_op jit(solution)/shard_map/all_to_all | solution.py:88
  35.2 1.6 fusion.8
  36.7 9.6 %all-to-all-done.1 = bf16[32,16,512]{2,1,0:T(8,128)(2,1)S(1)} async-done(((bf16[32,16,512]{2,1,0:T(8,128)(2,1)}), bf16[32,16,512]{2,1,0:T(8,128)(2,1)S(1)}, u32[]{:S(2)}, u32[]{:S(2)}) %all-to-all-start.1) | async-done | bytes 524320 | tf_op jit(solution)/shard_map/all_to_all | solution.py:88
  46.3 5.3 %gather_fusion.1 = bf16[1024,512]{1,0:T(8,128)(2,1)} fusion(bf16[512,512]{1,0:T(8,128)(2,1)S(1)} %bitcast.72, s32[1024]{0:T(1024)S(1)} %fusion.35), kind=kCustom, calls=%fused_computation.1 | custom fusion | bytes 2101248 | tf_op jit(solution)/shard_map/gather | solution.py:92
  53.1 1.7 fusion.13
  54.8 8.6 %fusion.42 = (bf16[1024,2048]{1,0:T(8,128)(2,1)S(1)}, f32[1024,2048]{1,0:T(8,128)}, f32[1024,2048]{1,0:T(8,128)}) fusion(bf16[512,2048]{1,0:T(8,128)(2,1)S(1)} %copy-done, bf16[1024,512]{1,0:T(8,128)(2,1)} %gather_fusion.1, f32[1024]{0:T(1024)S(1)} %fusion.36, f32[1024]{0:T(1024)S(1)} %broadcast_multiply_fusion.1), kind=kOutput, calls=%fused_computation.91 | convolution fusion | flops 2160066560 | bytes 24125440 | tf_op jit(solution)/shard_map/jvp()/dot_general | solution.py:45
  63.4 1.7 slice_bitcast_fusion
  65.1 2.3 copy.99
  68.7 11.8 %select_convert_fusion = (bf16[4,1024,1024]{2,1,0:T(8,128)(2,1)S(1)}, f32[4,1024,1024]{2,1,0:T(8,128)}) fusion(pred[1024,1024]{1,0:T(8,128)(4,1)} %fusion.8, bf16[1024,4,128]{0,2,1:T(8,128)(2,1)} %bitcast.84, bf16[1024,4,128]{0,2,1:T(8,128)(2,1)} %bitcast.82), kind=kOutput, calls=%fused_computation.8 | convolution fusion | flops 1107296256 | bytes 28311552 | tf_op jit(solution)/shard_map/jvp(ihd,jhd->hij)/dot_general | solution.py:60
  80.4 2.9 fusion.44
  85.2 2.9 copy.91
  88.1 3.4 %multiply_reduce_fusion = (f32[1024]{0:T(1024)S(1)}, bf16[1024,512]{1,0:T(8,128)(2,1)S(1)}) fusion(f32[1024,512]{1,0:T(8,128)} %copy.91, f32[1024,2048]{1,0:T(8,128)} %get-tuple-element.7, f32[1024]{0:T(1024)S(1)} %broadcast_multiply_fusion, bf16[1024,512]{1,0:T(8,128)(2,1)S(1)} %copy-done.9, bf16[512,512]{1,0:T(8,128)(2,1)} %param.12), kind=kOutput, calls=%fused_computation.47 | convolution fusion | flops 540015616 | bytes 6823936 | tf_op jit(solution)/shard_map/transpose(jvp())/dot_general | solution.py:73
  91.6 3.6 %fusion.41 = (f32[1024]{0:T(1024)S(1)}, f32[1024,512]{1,0:T(8,128)S(1)}, bf16[1024,512]{1,0:T(8,128)(2,1)}, f32[1024,512]{1,0:T(8,128)}) fusion(f32[1024]{0:T(1024)S(1)} %get-tuple-element.13, f32[1024,512]{1,0:T(8,128)S(1)} %copy-done.3, f32[1024]{0:T(1024)S(1)} %broadcast_multiply_fusion, f32[1024]{0:T(1024)S(1)} %get-tuple-element.14, ...), kind=kLoop, calls=%fused_computation.90 | loop fusion | flops 6290432 | bytes 10502144 | tf_op jit(solution)/shard_map/transpose(jvp())/reduce_sum | solution.py:36
  95.4 1.8 copy.92
  97.2 5.1 %fusion.45 = bf16[4,128,1024]{2,1,0:T(8,128)(2,1)S(1)} fusion(bf16[4,128,1024]{2,1,0:T(8,128)(2,1)} %bitcast.79, bf16[4,1024,1024]{2,1,0:T(8,128)(2,1)} %copy-done.1), kind=kOutput, calls=%fused_computation.93 | convolution fusion | flops 1073741824 | bytes 10485760 | tf_op jit(solution)/shard_map/transpose(jvp(hij,jhd->ihd))/dot_general | solution.py:68
  102.4 14.4 %fusion.2 = bf16[4,1024,1024]{2,1,0:T(8,128)(2,1)} fusion(f32[4,1024,1024]{2,1,0:T(8,128)} %get-tuple-element.17, pred[1024,1024]{1,0:T(8,128)(4,1)S(1)} %copy-done.13, bf16[4,128,1024]{2,1,0:T(8,128)(2,1)S(1)} %bitcast.80, bf16[128,4,8,128]{3,2,1,0:T(8,128)(2,1)S(1)} %copy-done.12), kind=kOutput, calls=%fused_computation.7 | convolution fusion | flops 1136656384 | bytes 28311552 | tf_op jit(solution)/shard_map/transpose(jvp(hij,jhd->ihd))/dot_general | solution.py:68
  116.8 7.4 %fusion.46 = bf16[4,1024,128]{1,2,0:T(8,128)(2,1)} fusion(bf16[4,1024,1024]{2,1,0:T(8,128)(2,1)} %fusion.2, bf16[1024,4,128]{0,2,1:T(8,128)(2,1)S(1)} %bitcast.83), kind=kOutput, calls=%fused_computation.94 | convolution fusion | flops 1073741824 | bytes 10485760 | tf_op jit(solution)/shard_map/transpose(jvp(ihd,jhd->hij))/dot_general | solution.py:60
  124.2 5.6 %fusion.47 = bf16[4,1024,128]{1,2,0:T(8,128)(2,1)} fusion(bf16[4,1024,1024]{2,1,0:T(8,128)(2,1)} %fusion.2, bf16[1024,4,128]{0,2,1:T(8,128)(2,1)S(1)} %bitcast.85), kind=kOutput, calls=%fused_computation.95 | convolution fusion | flops 1073741824 | bytes 10485760 | tf_op jit(solution)/shard_map/transpose(jvp(ihd,jhd->hij))/dot_general | solution.py:60
  131.1 2.4 copy.93
  133.5 2.3 copy.94
  135.8 2.8 convolution_convert_fusion.6
  138.5 2.2 reshape.242
  140.7 7.0 %fusion.4 = bf16[1024,2048]{1,0:T(8,128)(2,1)S(1)} fusion(f32[1024,2048]{1,0:T(8,128)} %get-tuple-element.15, f32[1024,512]{1,0:T(8,128)} %get-tuple-element.12, bf16[1024,512]{1,0:T(8,128)(2,1)} %copy.95, bf16[1024,512]{1,0:T(8,128)(2,1)} %copy.94, bf16[1024,512]{1,0:T(8,128)(2,1)} %copy.93), kind=kLoop, calls=%fused_computation.12 | loop fusion | flops 33554432 | bytes 17825792 | tf_op jit(solution)/shard_map/transpose(jvp(jit(silu)))/add_any | solution.py:45
  147.7 2.0 copy-done.6
  149.7 3.9 %convolution_convert_fusion = bf16[512,2048]{1,0:T(8,128)(2,1)} fusion(bf16[1024,2048]{1,0:T(8,128)(2,1)S(1)} %fusion.4, bf16[1024,512]{1,0:T(8,128)(2,1)S(1)} %copy-done.2, f32[1024]{0:T(1024)S(1)} %fusion.36, f32[1024]{0:T(1024)S(1)} %broadcast_multiply_fusion.1), kind=kOutput, calls=%fused_computation.28 | convolution fusion | flops 2149580800 | bytes 7348224 | tf_op jit(solution)/shard_map/transpose(jvp())/dot_general | solution.py:45
  153.5 4.5 %reshape.241 = bf16[128,8192]{1,0:T(8,128)(2,1)} reshape(bf16[512,2048]{1,0:T(8,128)(2,1)} %convolution_convert_fusion) | data formatting | bytes 4194304 | tf_op jit(solution)/shard_map/reshape | solution.py:117
  158.1 3.5 %maximum_bitcast_fusion = bf16[128,1,10240]{2,0,1:T(8,128)(2,1)} fusion(bf16[128,2048]{1,0:T(8,128)(2,1)} %reshape.242, bf16[128,8192]{1,0:T(8,128)(2,1)} %reshape.241), kind=kLoop, calls=%fused_computation.32 | loop fusion | flops 5242880 | bytes 5242880 | tf_op jit(solution)/shard_map/all_to_all | solution.py:16
  162.1 5.1 %reduce.9 = bf16[128,10240]{1,0:T(8,128)(2,1)} reduce(bf16[128,1,10240]{2,0,1:T(8,128)(2,1)} %maximum_bitcast_fusion, bf16[]{:T(256)} %broadcast.178), dimensions={1}, to_apply=%copy.87.reduce_sub_computation | reduce | bytes 5242882 | tf_op jit(solution)/shard_map/all_to_all | solution.py:16
  167.2 4.9 %reshape.306 = bf16[128,2,5120]{2,1,0:T(2,128)(2,1)} reshape(bf16[128,10240]{1,0:T(8,128)(2,1)} %reduce.9) | data formatting | bytes 5242880
  172.1 42.3 %all_to_all.35 = bf16[128,2,5120]{2,1,0:T(2,128)(2,1)} all-to-all(bf16[128,2,5120]{2,1,0:T(2,128)(2,1)} %reshape.306), channel_id=1, replica_groups=mesh['emb'=32,'seq'=4] {'emb','seq'}, dimensions={0} | all-to-all | bytes 5242880 | tf_op jit(solution)/shard_map/all_to_all | solution.py:16
  214.4 16.3 %reshape.307 = bf16[128,1,10240]{2,1,0:T(2,128)(2,1)} reshape(bf16[128,2,5120]{2,1,0:T(2,128)(2,1)} %all_to_all.35) | data formatting | bytes 5242880
  230.7 4.0 %copy.114 = bf16[128,1,10240]{2,0,1:T(8,128)(2,1)S(1)} copy(bf16[128,1,10240]{2,1,0:T(2,128)(2,1)} %reshape.307) | data formatting | bytes 5242880
  235.8 4.6 %fusion.15 = (f32[1024]{0:T(1024)S(1)}, bf16[1024,512]{1,0:T(8,128)(2,1)S(1)}) fusion(bf16[1024,512]{1,0:T(8,128)(2,1)S(1)} %copy-done.2, f32[1024]{0:T(1024)S(1)} %broadcast_multiply_fusion.1, bf16[1024,2048]{1,0:T(8,128)(2,1)} %copy-done.6, bf16[512,2048]{1,0:T(8,128)(2,1)S(1)} %copy-done), kind=kOutput, calls=%fused_computation.37 | convolution fusion | flops 2150104064 | bytes 8396800 | tf_op jit(solution)/shard_map/transpose(jvp())/dot_general | solution.py:45
  242.5 9.1 %scatter_custom_fusion = f32[512,512]{1,0:T(8,128)} fusion(s32[1024]{0:T(1024)S(1)} %copy-done.16, bf16[1024,512]{1,0:T(8,128)(2,1)} %param.13, bf16[1024,512]{1,0:T(8,128)(2,1)S(1)} %copy-done.2, bf16[1024,512]{1,0:T(8,128)(2,1)} %copy-done.7, f32[1024]{0:T(1024)S(1)} %negate_multiply_fusion, f32[1024]{0:T(1024)S(1)} %multiply_multiply_fusion, ...), kind=kCustom, calls=%fused_computation.44 | custom fusion | flops 6291456 | bytes 4210692 | tf_op jit(solution)/shard_map/scatter-add | solution.py:100
  251.6 2.1 convert_element_type.151
  253.6 4.4 %all-to-all-start.2 = ((bf16[32,16,512]{2,1,0:T(8,128)(2,1)}), bf16[32,16,512]{2,1,0:T(8,128)(2,1)}, u32[]{:S(2)}, u32[]{:S(2)}) async-start(bf16[32,16,512]{2,1,0:T(8,128)(2,1)} %bitcast.81), calls=%async_computation.2 | async-start | bytes 1048576 | tf_op jit(solution)/shard_map/all_to_all | solution.py:103
  259.4 10.8 %all-to-all-done.2 = bf16[32,16,512]{2,1,0:T(8,128)(2,1)} async-done(((bf16[32,16,512]{2,1,0:T(8,128)(2,1)}), bf16[32,16,512]{2,1,0:T(8,128)(2,1)}, u32[]{:S(2)}, u32[]{:S(2)}) %all-to-all-start.2) | async-done | bytes 524320 | tf_op jit(solution)/shard_map/all_to_all | solution.py:103
  270.2 8.1 %scatter_custom_fusion.1 = f32[4096,512]{1,0:T(8,128)} fusion(s32[512]{0:T(512)S(1)} %reshape.279, f32[]{:T(128)} %constant.38.clone.1, bf16[512,512]{1,0:T(8,128)(2,1)} %bitcast.25), kind=kCustom, calls=%fused_computation.15 | custom fusion | flops 524288 | bytes 8912900 | tf_op jit(solution)/shard_map/scatter-add | solution.py:110
  278.2 5.9 %convert_element_type.153 = bf16[4096,512]{1,0:T(8,128)(2,1)} convert(f32[4096,512]{1,0:T(8,128)} %scatter_custom_fusion.1) | non-fusion elementwise | flops 2097152 | bytes 12582912 | tf_op jit(solution)/shard_map/convert_element_type | solution.py:114
  284.1 3.0 fusion.16
  287.1 22.7 %all-gather.3.cloned.1.call-done = bf16[128,1,10240]{2,1,0:T(2,128)(2,1)} async-done(((bf16[1,1,10240]{2,1,0:T(2,128)(2,1)}), bf16[128,1,10240]{2,1,0:T(2,128)(2,1)}) %all-gather.3.cloned.1.call-update) | async-done | bytes 2621456 | tf_op jit(solution)/shard_map/all_gather | solution.py:28
  309.9 4.0 %copy.113 = bf16[128,1,10240]{2,0,1:T(8,128)(2,1)S(1)} copy(bf16[128,1,10240]{2,1,0:T(2,128)(2,1)} %all-gather.3.cloned.1.call-done) | data formatting | bytes 5242880
  316.7 3.9 %slice_convert_fusion = f32[128,8192]{1,0:T(8,128)} fusion(bf16[128,10240]{1,0:T(8,128)(2,1)} %bitcast.75), kind=kLoop, calls=%fused_computation.39 | loop fusion | flops 1048576 | bytes 6291456 | tf_op jit(solution)/shard_map/reshape | solution.py:133
  320.6 5.3 %reshape.250 = f32[512,2048]{1,0:T(8,128)} reshape(f32[128,8192]{1,0:T(8,128)} %slice_convert_fusion) | data formatting | bytes 8388608 | tf_op jit(solution)/shard_map/reshape | solution.py:133
  325.9 3.5 %reduce-scatter.2.cloned.1.call-done = bf16[1024,512]{1,0:T(8,128)(2,1)} async-done(((bf16[4096,512]{1,0:T(8,128)(2,1)}), bf16[1024,512]{1,0:T(8,128)(2,1)}) %reduce-scatter.2.cloned.1.call-update) | async-done | bytes 1048592 | tf_op jit(solution)/shard_map/reduce_scatter | solution.py:113
  329.4 2.8 convert_element_type.154
  (70 shorter events, 15.4 us)
Async XLA Ops:
  8.0 46.8 %copy-start = (bf16[512,2048]{1,0:T(8,128)(2,1)S(1)}, bf16[512,2048]{1,0:T(8,128)(2,1)}, u32[]{:S(2)}) copy-start(bf16[512,2048]{1,0:T(8,128)(2,1)} %param.11) | copy-start | bytes 6291460
  8.0 26.8 %copy-start.16 = (s32[1024]{0:T(1024)S(1)}, s32[1024]{0:T(1024)}, u32[]{:S(2)}) copy-start(s32[1024]{0:T(1024)} %param.9) | copy-start | bytes 12292
  8.0 26.9 %copy-start.17 = (s32[1,8]{1,0:T(1,128)S(1)}, s32[1,8]{1,0:T(1,128)}, u32[]{:S(2)}) copy-start(s32[1,8]{1,0:T(1,128)} %param.10) | copy-start | bytes 100
  30.6 15.7 %all-to-all-start.1 = ((bf16[32,16,512]{2,1,0:T(8,128)(2,1)}), bf16[32,16,512]{2,1,0:T(8,128)(2,1)S(1)}, u32[]{:S(2)}, u32[]{:S(2)}) async-start(bf16[32,16,512]{2,1,0:T(8,128)(2,1)} %bitcast.2), calls=%async_computation.1 | async-start | bytes 1048576 | tf_op jit(solution)/shard_map/all_to_all | solution.py:88
  34.8 275.1 %all-gather.3.cloned.1.call-start = ((), (), s32[]{:S(2)}) async-start(), calls=%async_computation.6 | async-start | bytes 5283840 | tf_op jit(solution)/shard_map/all_gather | solution.py:28
  68.7 11.8 %copy-start.11 = (bf16[128,4,8,128]{3,2,1,0:T(8,128)(2,1)S(1)}, bf16[128,4,8,128]{3,2,1,0:T(8,128)(2,1)}, u32[]{:S(2)}) copy-start(bf16[128,4,8,128]{3,2,1,0:T(8,128)(2,1)} %get-tuple-element.9) | copy-start | bytes 3145732
  80.4 3.2 copy-start.1
  83.6 1.3 copy-start.4
  83.6 4.5 %copy-start.9 = (bf16[1024,512]{1,0:T(8,128)(2,1)S(1)}, bf16[1024,512]{1,0:T(8,128)(2,1)}, u32[]{:S(2)}) copy-start(bf16[1024,512]{1,0:T(8,128)(2,1)} %param.13) | copy-start | bytes 3145732
  88.1 3.4 %copy-start.3 = (f32[1024,512]{1,0:T(8,128)S(1)}, f32[1024,512]{1,0:T(8,128)}, u32[]{:S(2)}) copy-start(f32[1024,512]{1,0:T(8,128)} %copy.91) | copy-start | bytes 6291460
  97.2 5.2 %copy-start.8 = (bf16[1024,512]{0,1:T(8,128)(2,1)S(1)}, bf16[1024,512]{0,1:T(8,128)(2,1)}, u32[]{:S(2)}) copy-start(bf16[1024,512]{0,1:T(8,128)(2,1)} %copy.92) | copy-start | bytes 3145732
  97.2 5.2 %copy-start.12 = (bf16[128,4,8,128]{3,2,1,0:T(8,128)(2,1)S(1)}, bf16[128,4,8,128]{3,2,1,0:T(8,128)(2,1)}, u32[]{:S(2)}) copy-start(bf16[128,4,8,128]{3,2,1,0:T(8,128)(2,1)} %get-tuple-element.9) | copy-start | bytes 3145732
  97.2 5.2 %copy-start.13 = (pred[1024,1024]{1,0:T(8,128)(4,1)S(1)}, pred[1024,1024]{1,0:T(8,128)(4,1)}, u32[]{:S(2)}) copy-start(pred[1024,1024]{1,0:T(8,128)(4,1)} %fusion.8) | copy-start | bytes 3145732
  102.4 14.4 %copy-start.14 = (bf16[1024,512]{0,1:T(8,128)(2,1)S(1)}, bf16[1024,512]{0,1:T(8,128)(2,1)}, u32[]{:S(2)}) copy-start(bf16[1024,512]{0,1:T(8,128)(2,1)} %copy.99) | copy-start | bytes 3145732
  116.8 7.4 %copy-start.15 = (bf16[1024,512]{0,1:T(8,128)(2,1)S(1)}, bf16[1024,512]{0,1:T(8,128)(2,1)}, u32[]{:S(2)}) copy-start(bf16[1024,512]{0,1:T(8,128)(2,1)} %copy.98) | copy-start | bytes 3145732
  131.1 4.7 %copy-start.10 = (bf16[1024,512]{1,0:T(8,128)(2,1)S(1)}, bf16[1024,512]{1,0:T(8,128)(2,1)}, u32[]{:S(2)}) copy-start(bf16[1024,512]{1,0:T(8,128)(2,1)} %param.13) | copy-start | bytes 3145732
  140.7 9.0 %copy-start.2 = (bf16[1024,512]{1,0:T(8,128)(2,1)S(1)}, bf16[1024,512]{1,0:T(8,128)(2,1)}, u32[]{:S(2)}) copy-start(bf16[1024,512]{1,0:T(8,128)(2,1)} %gather_fusion.1) | copy-start | bytes 3145732
  147.7 2.0 copy-start.6
  240.5 1.0 copy-start.7
  253.6 16.5 %all-to-all-start.2 = ((bf16[32,16,512]{2,1,0:T(8,128)(2,1)}), bf16[32,16,512]{2,1,0:T(8,128)(2,1)}, u32[]{:S(2)}, u32[]{:S(2)}) async-start(bf16[32,16,512]{2,1,0:T(8,128)(2,1)} %bitcast.81), calls=%async_computation.2 | async-start | bytes 1048576 | tf_op jit(solution)/shard_map/all_to_all | solution.py:103
  258.0 71.4 %reduce-scatter.2.cloned.1.call-start = ((), (), s32[]{:S(2)}) async-start(), calls=%async_computation.5 | async-start | bytes 5242880 | tf_op jit(solution)/shard_map/reduce_scatter | solution.py:113
  313.8 1.5 copy-start.5
Sparse Core Ops, SparseCore 0:
  235.9 73.8 all-gather.2
Sparse Core Ops, SparseCore 1:
  284.2 45.2 reduce-scatter.1
where the time goes:
time: 345 us; the launch traced here: 340 us
  local copies, waits for them, and re-layouts  77.1 us (22%)
  matrix products  73.5 us (21%)
  other arithmetic  59.5 us (17%)
  blocking collectives  58.5 us (17%)
  waiting for transfers between devices  46.7 us (14%)
  between operations  16 us (5%)
  starting transfers between devices  8.68 us (3%)
    all_to_all x1, blocking collectives, in_one_piece(): lax.all_to_all(both, axis, split_axis=split_dim, concat_axis=concat_dim,...  42.3 us
    unnamed x42, local copies, waits for them, and re-layouts  37.8 us
    dot_general x3, matrix products, hstu_layer(): jnp.einsum('ihd,jhd->hij', queries, key_rows, preferred_element_type=jnp....  24.7 us
    all_gather x1, waiting for transfers between devices, in_one_piece_2(): out, at, done = (lax.all_gather(both, axis, axis=dim, tiled=True), 0, [])  22.7 us
    dot_general x3, matrix products, hstu_layer(): jnp.einsum('hij,jhd->ihd', weights, values, preferred_element_type=jnp.fl...  22.4 us
    dot_general x3, matrix products, hstu_layer(): jnp.dot(normed, in_weight, preferred_element_type=jnp.float32)  17.1 us
    all_to_all x1, blocking collectives, on_device(): lax.all_to_all(requests, 'emb', split_axis=0, concat_axis=0, tiled=True)  16.2 us
    all_to_all x1, waiting for transfers between devices, on_device(): lax.all_to_all(slot_grad.reshape(emb_count, -1, model_width).astype(jnp.b...  10.8 us
  transfers between devices with their start and end apart: 4, of which 4 were waited for; matrix products, arithmetic and copies ran while one was open for 15% of the time, Pallas kernels for 0%

commit v1 on v0

v1 whole, which is shorter than its diff:
```python
import functools, math
import jax, jax.numpy as jnp
from jax import lax
from jax.experimental import pallas as pl
from jax.experimental.pallas import tpu as pltpu
from jax.sharding import PartitionSpec as P

F32, BF16 = jnp.float32, jnp.bfloat16
EPS = 1e-05
MOST = 512
B = 256
LAST = (((1,), (1,)), ((), ()))


def rows_at(i):
    return pl.ds(pl.multiple_of(i * B, B), B)


def expand(ev_ref, tab_ref, events_s, pick_s):
    slots = tab_ref.shape[0]
    ev = ev_ref[...]
    ev_t = jnp.transpose(ev)
    lane = lax.broadcasted_iota(jnp.int32, (128, slots), 1)
    sub = lax.broadcasted_iota(jnp.int32, (slots, 128), 0)
    for a in range(ev.shape[0]):
        hot = jnp.where(ev_t[:, a : a + 1] == lane, 1.0, 0.0).astype(BF16)
        events_s[128 * a : 128 * a + 128, :] = jnp.dot(
            hot, tab_ref[...], preferred_element_type=F32
        ).astype(BF16)
        pick_s[:, 128 * a : 128 * a + 128] = jnp.where(sub == ev[a : a + 1, :], 1.0, 0.0).astype(
            BF16
        )


def project(r, events_s, win_ref, normed_s, normed_t, rstd_s, gate_s, dsil_s, qkv_s, kv_t):
    rows = rows_at(r)
    width = events_s.shape[1]
    e = events_s[rows, :].astype(F32)
    c = e - jnp.mean(e, axis=-1, keepdims=True)
    rs = lax.rsqrt(jnp.mean(c * c, axis=-1, keepdims=True) + EPS)
    n = (c * rs).astype(BF16)
    normed_s[rows, :] = n
    rstd_s[rows, :] = rs
    normed_t[:, rows] = jnp.transpose(n)
    for b in range(4):
        cols = slice(b * width, (b + 1) * width)
        x = jnp.dot(n, win_ref[:, cols], preferred_element_type=F32)
        hx = 0.5 * x
        t = jnp.tanh(hx)
        u = 1.0 + t
        y = hx * u
        dsil_s[rows, cols] = (0.5 * (u + hx * (1.0 - t * t))).astype(BF16)
        if b == 0:
            gate_s[rows, :] = y
        else:
            yb = y.astype(BF16)
            qkv_s[b - 1, rows, :] = yb
            if b == 1:
                kv_t[1, :, rows] = jnp.transpose(yb)
            elif b == 3:
                kv_t[0, :, rows] = jnp.transpose(yb)


def pairs(blocks):
    back = MOST // B
    return [(q, k) for q in range(blocks) for k in range(max(0, q - back), q + 1)]


def attend(h, starts, qkv_s, kv_t, att_t, p_s, d_s, blocks):
    hc = pl.ds(pl.multiple_of(h * 128, 128), 128)
    lane = lax.broadcasted_iota(jnp.int32, (B, B), 1)
    sub = lax.broadcasted_iota(jnp.int32, (B, B), 0)
    head = 128
    c1 = 0.5 / math.sqrt(head)
    total = None
    for i, (q, k) in enumerate(pairs(blocks)):
        kk = qkv_s[2, k * B : (k + 1) * B, hc]
        qq = qkv_s[1, q * B : (q + 1) * B, hc]
        x = lax.dot_general(kk, qq, LAST, preferred_element_type=F32)
        hh = x * c1
        t = jnp.tanh(hh)
        u = 1.0 + t
        mask = (sub + k * B) >= starts[q]
        if q == k:
            mask = mask & (sub <= lane)
        w = jnp.where(mask, (hh * u) * (1.0 / MOST), 0.0).astype(BF16)
        d = jnp.where(mask, (u + hh * (1.0 - t * t)) * (c1 / MOST), 0.0).astype(BF16)
        p_s[h, i] = w
        d_s[h, i] = d
        o = jnp.dot(kv_t[1, hc, k * B : (k + 1) * B], w, preferred_element_type=F32)
        total = o if k == max(0, q - MOST // B) else total + o
        if q == k:
            att_t[hc, q * B : (q + 1) * B] = total


def middle(r, att_t, gate_s, dsil_s, events_s, wout_ref, og_ref, lo_ref, gated_t, dx_s, do_s):
    rows = rows_at(r)
    width = events_s.shape[1]
    a = jnp.transpose(att_t[:, rows])
    c = a - jnp.mean(a, axis=-1, keepdims=True)
    rs = lax.rsqrt(jnp.mean(c * c, axis=-1, keepdims=True) + EPS)
    xh = c * rs
    gate = gate_s[rows, :]
    gated = (xh * gate).astype(BF16)
    out = jnp.dot(gated, wout_ref[...], preferred_element_type=F32)
    lo_ref[rows, :] = (out + events_s[rows, :].astype(F32)).astype(BF16)
    gated_t[:, rows] = jnp.transpose(gated)
    og = og_ref[rows, :]
    dg = lax.dot_general(og, wout_ref[...], LAST, preferred_element_type=F32)
    dg = dg.astype(BF16).astype(F32)
    dx_s[rows, :width] = (dg * xh * dsil_s[rows, :width].astype(F32)).astype(BF16)
    dxh = dg * gate
    m1 = jnp.mean(dxh, axis=-1, keepdims=True)
    m2 = jnp.mean(dxh * xh, axis=-1, keepdims=True)
    do_s[rows, :] = (rs * (dxh - m1 - xh * m2)).astype(BF16)


def attend_back(h, qkv_s, kv_t, p_s, d_s, do_s, dsil_s, dx_s, dq_t, blocks, width):
    hc = pl.ds(pl.multiple_of(h * 128, 128), 128)

    def put(block, part, grad):
        cols = pl.ds(pl.multiple_of(part * width + h * 128, 128), 128)
        rows = slice(block * B, (block + 1) * B)
        dx_s[rows, cols] = (
            grad.astype(BF16).astype(F32) * dsil_s[rows, cols].astype(F32)
        ).astype(BF16)

    order = pairs(blocks)
    for k in range(blocks):
        dv = dk = None
        vv = qkv_s[0, k * B : (k + 1) * B, hc]
        for q in range(k, min(k + MOST // B, blocks - 1) + 1):
            i = order.index((q, k))
            do = do_s[q * B : (q + 1) * B, hc]
            dp = lax.dot_general(vv, do, LAST, preferred_element_type=F32).astype(BF16)
            ds = dp * d_s[h, i]
            dv1 = jnp.dot(p_s[h, i], do, preferred_element_type=F32)
            dk1 = jnp.dot(ds, qkv_s[1, q * B : (q + 1) * B, hc], preferred_element_type=F32)
            dv = dv1 if dv is None else dv + dv1
            dk = dk1 if dk is None else dk + dk1
            dq1 = jnp.dot(kv_t[0, hc, k * B : (k + 1) * B], ds, preferred_element_type=F32)
            at = slice(q * B, (q + 1) * B)
            if k == max(0, q - MOST // B):
                dq_t[:, at] = dq1
            else:
                dq_t[:, at] += dq1
        put(k, 1, dv)
        put(k, 3, dk)
    for q in range(blocks):
        put(q, 2, jnp.transpose(dq_t[:, q * B : (q + 1) * B]))


def event_back(r, dx_s, win_ref, normed_s, rstd_s, og_ref, eg_s):
    rows = rows_at(r)
    g = lax.dot_general(dx_s[rows, :], win_ref[...], LAST, preferred_element_type=F32)
    g = g.astype(BF16).astype(F32)
    xh = normed_s[rows, :].astype(F32)
    m1 = jnp.mean(g, axis=-1, keepdims=True)
    m2 = jnp.mean(g * xh, axis=-1, keepdims=True)
    de = (rstd_s[rows, :] * (g - m1 - xh * m2)).astype(BF16)
    eg_s[rows, :] = (de.astype(F32) + og_ref[rows, :].astype(F32)).astype(BF16)


def row_starts(len_ref, blocks):
    ends, at = [], jnp.int32(0)
    for s in range(len_ref.shape[1]):
        at = at + len_ref[0, s]
        ends.append(at)
    starts = []
    for q in range(blocks):
        place = lax.broadcasted_iota(jnp.int32, (1, B), 1) + q * B
        start = jnp.zeros((1, B), jnp.int32)
        for e in ends:
            start = jnp.where(place >= e, e, start)
        starts.append(start)
    return starts


def compute(len_ref, ev_ref, tab_ref, win_ref, wout_ref, og_ref, lo_ref, sg_ref, g_ref,
            events_s, pick_s, normed_s, normed_t, rstd_s, gate_s, dsil_s, qkv_s, kv_t,
            att_t, p_s, d_s, gated_t, dx_s, do_s, dq_t, eg_s):
    tokens, width = og_ref.shape
    blocks = tokens // B
    heads = width // 128
    expand(ev_ref, tab_ref, events_s, pick_s)
    pl.loop(0, blocks)(lambda r: project(
        r, events_s, win_ref, normed_s, normed_t, rstd_s, gate_s, dsil_s, qkv_s, kv_t))
    starts = row_starts(len_ref, blocks)
    pl.loop(0, heads)(lambda h: attend(h, starts, qkv_s, kv_t, att_t, p_s, d_s, blocks))
    pl.loop(0, blocks)(lambda r: middle(
        r, att_t, gate_s, dsil_s, events_s, wout_ref, og_ref, lo_ref, gated_t, dx_s, do_s))

    def put_grad(c, val):
        g_ref[pl.ds(c * 64, 32)] = val[:, :128].astype(BF16).reshape(32, 16, 128)
        g_ref[pl.ds(c * 64 + 32, 32)] = val[:, 128:].astype(BF16).reshape(32, 16, 128)

    for c in range(2):
        put_grad(8 + c, jnp.dot(gated_t[...], og_ref[:, c * B : (c + 1) * B],
                                preferred_element_type=F32))
    pl.loop(0, heads)(lambda h: attend_back(
        h, qkv_s, kv_t, p_s, d_s, do_s, dsil_s, dx_s, dq_t, blocks, width))
    pl.loop(0, blocks)(lambda r: event_back(r, dx_s, win_ref, normed_s, rstd_s, og_ref, eg_s))
    sg_ref[...] = jnp.dot(pick_s[...], eg_s[...], preferred_element_type=F32).astype(BF16)

    @pl.loop(0, 8)
    def _(c):
        cols = pl.ds(pl.multiple_of(c * B, B), B)
        put_grad(c, jnp.dot(normed_t[...], dx_s[:, cols], preferred_element_type=F32))


def compute_scratch(tokens, width, slots):
    n = len(pairs(tokens // B))
    heads = width // 128
    return [
        pltpu.VMEM((tokens, width), BF16),
        pltpu.VMEM((slots, tokens), BF16),
        pltpu.VMEM((tokens, width), BF16),
        pltpu.VMEM((width, tokens), BF16),
        pltpu.VMEM((tokens, 1), F32),
        pltpu.VMEM((tokens, width), F32),
        pltpu.VMEM((tokens, 4 * width), BF16),
        pltpu.VMEM((3, tokens, width), BF16),
        pltpu.VMEM((2, width, tokens), BF16),
        pltpu.VMEM((width, tokens), F32),
        pltpu.VMEM((heads, n, B, B), BF16),
        pltpu.VMEM((heads, n, B, B), BF16),
        pltpu.VMEM((width, tokens), BF16),
        pltpu.VMEM((tokens, 4 * width), BF16),
        pltpu.VMEM((tokens, width), BF16),
        pltpu.VMEM((128, tokens), F32),
        pltpu.VMEM((tokens, width), BF16),
    ]


def local_layer(lengths, ev, tab, win, wout, og):
    tokens, width = og.shape
    slots = tab.shape[0]
    vm = pl.BlockSpec(memory_space=pltpu.VMEM)
    return pl.pallas_call(
        compute,
        name="layer",
        out_shape=(
            jax.ShapeDtypeStruct((tokens, width), BF16),
            jax.ShapeDtypeStruct((slots, width), BF16),
            jax.ShapeDtypeStruct((640, 16, 128), BF16),
        ),
        in_specs=[pl.BlockSpec(memory_space=pltpu.SMEM)] + [vm] * 5,
        out_specs=(vm, vm, vm),
        scratch_shapes=compute_scratch(tokens, width, slots),
        compiler_params=pltpu.CompilerParams(vmem_limit_bytes=64000000),
        cost_estimate=pl.CostEstimate(flops=14 * 10**9, bytes_accessed=8 * 10**6, transcendentals=6 * 10**6),
    )(lengths, ev, tab, win, wout, og)


MESH = pl.DeviceIdType.MESH


def remote(src, dst, send_sem, recv_sem, emb, seq):
    return pltpu.make_async_remote_copy(
        src_ref=src, dst_ref=dst, send_sem=send_sem, recv_sem=recv_sem,
        device_id=(emb, seq), device_id_type=MESH,
    )


def greet(peers):
    barrier = pltpu.get_barrier_semaphore()
    for emb, seq in peers:
        pl.semaphore_signal(barrier, inc=1, device_id=(emb, seq), device_id_type=MESH)
    pl.semaphore_wait(barrier, len(peers))


def fetch(n_emb, n_seq, req_ref, table_ref, tab_ref, idx_ref, table_v, rows_v, load_sem,
          i_send, i_recv, y_send, y_recv, r_send, r_recv):
    e, s = lax.axis_index("emb"), lax.axis_index("seq")
    load = pltpu.make_async_copy(table_ref, table_v, load_sem)
    load.start()
    greet([(lax.rem(e + d, n_emb), s) for d in range(1, n_emb)]
          + [(e, lax.rem(s + d, n_seq)) for d in range(1, n_seq)])

    def ask(d):
        to = lax.rem(e + d, n_emb)
        return remote(req_ref.at[to], idx_ref.at[s, e], i_send.at[d], i_recv.at[d], to, s)

    for d in range(1, n_emb):
        ask(d).start()
    idx_ref[s, e] = req_ref[e]
    for d in range(1, n_emb):
        ask(d).wait_recv()

    def tell(d):
        to = lax.rem(s + d, n_seq)
        return remote(idx_ref.at[s], idx_ref.at[s], y_send.at[d], y_recv.at[d], e, to)

    for d in range(1, n_seq):
        tell(d).start()
    load.wait()
    shard = table_v.shape[0]
    lane = lax.broadcasted_iota(jnp.int32, (128, shard), 1)
    cap = tab_ref.shape[0] // n_emb
    per = 128 // cap
    groups = n_emb // per
    mine = e // per

    def answer(g, i, j):
        to = g * per + i
        src = rows_v.at[j, pl.ds(pl.multiple_of(i * cap, cap), cap)]
        dst = tab_ref.at[pl.ds(pl.multiple_of(e * cap, cap), cap)]
        return remote(src, dst, r_send.at[to], r_recv.at[e], to, s)

    for j in (2, 1, 3, 0):
        g = lax.rem(mine + j, groups)
        row = idx_ref[s, g * per]
        for i in range(1, per):
            row = row + idx_ref[s, g * per + i]
        col = jnp.transpose(jnp.broadcast_to(row, (8, 128)))[:, 0:1]
        hot = jnp.where(col == lane, 1.0, 0.0).astype(BF16)
        rows_v[j] = jnp.dot(hot, table_v[...], preferred_element_type=F32).astype(BF16)
        for t in range(per):
            i = lax.rem(lax.rem(e, per) + t, per)
            if j == 0 and t == 0:
                tab_ref[pl.ds(pl.multiple_of(e * cap, cap), cap), :] = rows_v[
                    0, pl.ds(pl.multiple_of(i * cap, cap), cap), :]
            else:
                answer(g, i, j).start()
    for d in range(1, n_emb):
        frm = lax.rem(e + d, n_emb)
        remote(rows_v.at[0, pl.ds(0, cap)], tab_ref.at[pl.ds(pl.multiple_of(frm * cap, cap), cap)],
               r_send.at[frm], r_recv.at[frm], frm, s).wait_recv()
    for d in range(1, n_seq):
        tell(d).wait()
    for d in range(1, n_emb):
        ask(d).wait_send()
        frm = lax.rem(e + d, n_emb)
        remote(rows_v.at[0, pl.ds(0, cap)], tab_ref.at[pl.ds(0, cap)],
               r_send.at[frm], r_recv.at[frm], frm, s).wait_send()


def fetch_rows_of(req, table, n_emb, n_seq, slots):
    vm = pl.BlockSpec(memory_space=pltpu.VMEM)
    width = table.shape[1]
    return pl.pallas_call(
        functools.partial(fetch, n_emb, n_seq),
        name="fetch",
        out_shape=(
            jax.ShapeDtypeStruct((slots, width), BF16),
            jax.ShapeDtypeStruct((n_seq, n_emb, 1, 128), jnp.int32),
        ),
        in_specs=[vm, pl.BlockSpec(memory_space=pl.ANY)],
        out_specs=(vm, vm),
        scratch_shapes=[
            pltpu.VMEM(table.shape, BF16),
            pltpu.VMEM((4, 128, width), BF16),
            pltpu.SemaphoreType.DMA,
            pltpu.SemaphoreType.DMA((n_emb,)),
            pltpu.SemaphoreType.DMA((n_emb,)),
            pltpu.SemaphoreType.DMA((n_seq,)),
            pltpu.SemaphoreType.DMA((n_seq,)),
            pltpu.SemaphoreType.DMA((n_emb,)),
            pltpu.SemaphoreType.DMA((n_emb,)),
        ],
        compiler_params=pltpu.CompilerParams(
            collective_id=0, has_side_effects=True, vmem_limit_bytes=40000000),
    )(req, table)


def share(n_emb, n_seq, sg_ref, g_ref, all_ref, sum_ref, half_s, pair_s, b1, p_s, b2, b3,
          g_send, g_recv, y_send, y_recv, z_send, z_recv, w_send, w_recv):
    e, s = lax.axis_index("emb"), lax.axis_index("seq")
    c, x, z = lax.rem(e, 2), lax.rem(e // 2, 4), e // 8
    cap = sg_ref.shape[0] // n_emb
    units = g_ref.shape[0]
    half, part, piece, bit = units // 2, units // 4, units // 16, units // 64
    along = {0: (x, z), 1: (z, x)}

    def peer(color, step, at):
        if (color + step) % 2 == 0:
            return (z * 4 + at) * 2 + c
        return (at * 4 + x) * 2 + c

    other = e + 1 - 2 * c
    greet([(lax.rem(e + d, n_emb), s) for d in range(1, n_emb)]
          + [(e, lax.rem(s + d, n_seq)) for d in range(1, n_seq)])

    def halve(k, j):
        src = g_ref.at[pl.ds((1 - c) * half + k * part + j * piece, piece)]
        return remote(src, pair_s.at[k, j], w_send.at[0, k, j], w_recv.at[0, k, j], other, s)

    def swap_grad(d):
        to = lax.rem(e + d, n_emb)
        return remote(sg_ref.at[pl.ds(pl.multiple_of(to * cap, cap), cap)],
                      all_ref.at[s, pl.ds(pl.multiple_of(e * cap, cap), cap)],
                      g_send.at[d], g_recv.at[d], to, s)

    for j in range(4):
        for k in range(2):
            halve(k, j).start()
    for d in range(1, n_emb):
        swap_grad(d).start()
    own = pl.ds(pl.multiple_of(e * cap, cap), cap)
    all_ref[s, own, :] = sg_ref[own, :]

    def spread(k, d):
        m = along[k][0]
        to = lax.rem(m + d, 4)
        return remote(half_s.at[k, to], b1.at[k, m], w_send.at[1, k, d], w_recv.at[1, k, d],
                      peer(k, 0, to), s)

    for j in range(4):
        for k in range(2):
            halve(k, j).wait_recv()
    for k in range(2):
        for d in (2, 1, 3, 0):
            j = lax.rem(along[k][0] + d, 4)
            mine = g_ref[pl.ds(c * half + k * part + j * piece, piece)].astype(F32)
            half_s[k, j] = (mine + pair_s[k, j].astype(F32)).astype(BF16)
            if d:
                spread(k, d).start()

    chunk = all_ref.shape[1] // 4
    up, down = lax.rem(s + 1, n_seq), lax.rem(s + n_seq - 1, n_seq)
    far = lax.rem(s + 2, n_seq)

    def pass_on(q, way):
        rows = pl.ds(q * chunk, chunk)
        return remote(all_ref.at[s, rows], all_ref.at[s, rows], y_send.at[way, q],
                      y_recv.at[way, q], e, down if way else up)

    def relay(q):
        frm, to = (down, up) if q < 2 else (up, down)
        rows = pl.ds(q * chunk, chunk)
        return remote(all_ref.at[frm, rows], all_ref.at[frm, rows], z_send.at[q], z_recv.at[q],
                      e, to)

    for d in range(1, n_emb):
        swap_grad(d).wait_recv()
    early = (0, 2)
    late = (1, 3)
    for q in early:
        for way in range(2):
            pass_on(q, way).start()

    def spread2(k, d):
        m = along[k][1]
        to = lax.rem(m + d, 4)
        return remote(p_s.at[k, to], b2.at[k, m], w_send.at[2, k, d], w_recv.at[2, k, d],
                      peer(k, 1, to), s)

    for k in range(2):
        m = along[k][0]
        total = half_s[k, m].astype(F32)
        for d in range(1, 4):
            spread(k, d).wait_recv()
        for d in range(1, 4):
            total = total + b1[k, lax.rem(m + d, 4)].astype(F32)
        for j in range(4):
            p_s[k, j] = total[j * bit : (j + 1) * bit].astype(BF16)
        for d in (2, 1, 3):
            spread2(k, d).start()

    def gather3(k, d):
        to = lax.rem(s + d, n_seq)
        return remote(b3.at[k, s], b3.at[k, s], w_send.at[3, k, d], w_recv.at[3, k, d], e, to)

    for k in range(2):
        m = along[k][1]
        total = p_s[k, m].astype(F32)
        for d in range(1, 4):
            spread2(k, d).wait_recv()
        for d in range(1, 4):
            total = total + b2[k, lax.rem(m + d, 4)].astype(F32)
        b3[k, s] = total.astype(BF16)
        for d in range(1, 4):
            gather3(k, d).start()
    for q in early:
        pass_on(q, 0 if q < 2 else 1).wait_recv()
        relay(q).start()
    for q in late:
        for way in range(2):
            pass_on(q, way).start()

    def place(k, first, second):
        return c * half + k * part + first * piece + second * bit

    def back2(k, d):
        to = lax.rem(along[k][1] + d, 4)
        ref = sum_ref.at[pl.ds(place(k, *along[k]), bit)]
        return remote(ref, ref, w_send.at[4, k, d], w_recv.at[4, k, d], peer(k, 1, to), s)

    def back1(k, d):
        to = lax.rem(along[k][0] + d, 4)
        ref = sum_ref.at[pl.ds(place(k, along[k][0], 0), piece)]
        return remote(ref, ref, w_send.at[5, k, d], w_recv.at[5, k, d], peer(k, 0, to), s)

    def back0(k, d):
        j = lax.rem(along[k][0] + 4 - d, 4)
        ref = sum_ref.at[pl.ds(place(k, j, 0), piece)]
        return remote(ref, ref, w_send.at[6, k, d], w_recv.at[6, k, d], other, s)

    for k in range(2):
        for d in range(1, 4):
            gather3(k, d).wait_recv()
        total = b3[k, 0].astype(F32)
        for j in range(1, 4):
            total = total + b3[k, j].astype(F32)
        sum_ref[pl.ds(place(k, *along[k]), bit)] = total.astype(BF16)
        for d in range(1, 4):
            back2(k, d).start()
    for k in range(2):
        for d in range(1, 4):
            back2(k, d).wait_recv()
        for d in (2, 1, 3):
            back1(k, d).start()
        back0(k, 0).start()
    for q in late:
        pass_on(q, 0 if q < 2 else 1).wait_recv()
        relay(q).start()
    for d in (1, 3, 2):
        for k in range(2):
            back1(k, d).wait_recv()
            back0(k, d).start()
    for q in range(4):
        pass_on(q, 1 if q < 2 else 0).wait_recv()
        relay(q).wait_recv()
    for k in range(2):
        for d in range(4):
            back0(k, d).wait_recv()

    for k in range(2):
        for j in range(4):
            halve(k, j).wait_send()
            back0(k, j).wait_send()
        for d in range(1, 4):
            for copy in (spread, spread2, gather3, back2, back1):
                copy(k, d).wait_send()
    for d in range(1, n_emb):
        swap_grad(d).wait_send()
    for q in range(4):
        relay(q).wait_send()
        for way in range(2):
            pass_on(q, way).wait_send()


def share_grads(sg, g, n_emb, n_seq):
    vm = pl.BlockSpec(memory_space=pltpu.VMEM)
    slots, width = sg.shape
    units = g.shape[0]
    tile = g.shape[1:]
    dma = pltpu.SemaphoreType.DMA
    return pl.pallas_call(
        functools.partial(share, n_emb, n_seq),
        name="share",
        out_shape=(
            jax.ShapeDtypeStruct((n_seq, slots, width), BF16),
            jax.ShapeDtypeStruct(g.shape, BF16),
        ),
        in_specs=[vm, vm],
        out_specs=(vm, vm),
        scratch_shapes=[
            pltpu.VMEM((2, 4, units // 16) + tile, BF16),
            pltpu.VMEM((2, 4, units // 16) + tile, BF16),
            pltpu.VMEM((2, 4, units // 16) + tile, BF16),
            pltpu.VMEM((2, 4, units // 64) + tile, BF16),
            pltpu.VMEM((2, 4, units // 64) + tile, BF16),
            pltpu.VMEM((2, n_seq, units // 64) + tile, BF16),
            dma((n_emb,)), dma((n_emb,)),
            dma((2, 4)), dma((2, 4)), dma((4,)), dma((4,)),
            dma((7, 2, 4)), dma((7, 2, 4)),
        ],
        compiler_params=pltpu.CompilerParams(
            collective_id=1, has_side_effects=True, vmem_limit_bytes=40000000),
    )(sg, g)


def finish(n_seq, idx_ref, all_ref, sum_ref, tg_ref, wi_ref, wo_ref, pick_s, tg_v, wi_v, wo_v, sems):
    s = lax.axis_index("seq")
    width = all_ref.shape[2]
    shard = tg_ref.shape[0]
    for b in range(16):
        wi_v[:, b * 128 : (b + 1) * 128] = sum_ref[b * 32 : (b + 1) * 32].reshape(width, 128).astype(F32)
    put_in = pltpu.make_async_copy(wi_v, wi_ref, sems.at[0])
    put_in.start()
    for b in range(4):
        wo_v[:, b * 128 : (b + 1) * 128] = (
            sum_ref[512 + b * 32 : 544 + b * 32].reshape(width, 128).astype(F32))
    put_out = pltpu.make_async_copy(wo_v, wo_ref, sems.at[1])
    put_out.start()
    sub = lax.broadcasted_iota(jnp.int32, (shard, 128), 0) + s * shard
    groups = idx_ref.shape[1] // 8
    for q in range(n_seq):
        for g in range(groups):
            row = idx_ref[q, 8 * g]
            for i in range(1, 8):
                row = row + idx_ref[q, 8 * g + i]
            at = (q * groups + g) * 128
            pick_s[:, at : at + 128] = jnp.where(sub == row, 1.0, 0.0).astype(BF16)
    cand = all_ref[...].reshape(-1, width)
    step = shard // 4
    copies = []
    for b in range(4):
        rows = slice(b * step, (b + 1) * step)
        tg_v[rows, :] = jnp.dot(pick_s[rows, :], cand, preferred_element_type=F32)
        copies.append(pltpu.make_async_copy(tg_v.at[rows], tg_ref.at[rows], sems.at[2 + b]))
        copies[-1].start()
    put_in.wait()
    put_out.wait()
    for copy in copies:
        copy.wait()


def finish_grads(idx, every, total, shard, width):
    vm = pl.BlockSpec(memory_space=pltpu.VMEM)
    hbm = pl.BlockSpec(memory_space=pl.ANY)
    n_seq = every.shape[0]
    return pl.pallas_call(
        functools.partial(finish, n_seq),
        name="finish",
        out_shape=(
            jax.ShapeDtypeStruct((shard, width), F32),
            jax.ShapeDtypeStruct((width, 4 * width), F32),
            jax.ShapeDtypeStruct((width, width), F32),
        ),
        in_specs=[vm, vm, vm],
        out_specs=(hbm, hbm, hbm),
        scratch_shapes=[
            pltpu.VMEM((shard, n_seq * every.shape[1]), BF16),
            pltpu.VMEM((shard, width), F32),
            pltpu.VMEM((width, 4 * width), F32),
            pltpu.VMEM((width, width), F32),
            pltpu.SemaphoreType.DMA((6,)),
        ],
        compiler_params=pltpu.CompilerParams(vmem_limit_bytes=50000000),
    )(idx, every, total)


def on_device(item_table, fetch_rows, event_slot, lengths, in_weight, out_weight, out_grad):
    n_emb, n_seq = lax.axis_size("emb"), lax.axis_size("seq")
    cap = fetch_rows.shape[-1]
    asked = fetch_rows.reshape(n_emb, cap)
    place = lax.broadcasted_iota(jnp.int32, (n_emb, 128), 1) // cap
    req = jnp.where(place == lax.rem(lax.axis_index("emb"), 128 // cap),
                    jnp.tile(asked, (1, 128 // cap)), 0)
    tab, idx = fetch_rows_of(req.reshape(n_emb, 1, 128), item_table, n_emb, n_seq, n_emb * cap)
    layer_out, slot_grad, weight_grad = local_layer(
        lengths, event_slot.reshape(-1, 128), tab, in_weight, out_weight, out_grad)
    every, total = share_grads(slot_grad, weight_grad, n_emb, n_seq)
    table_grad, in_total, out_total = finish_grads(
        idx, every, total, item_table.shape[0] // n_seq, item_table.shape[1])
    return layer_out, table_grad, in_total, out_total


def solution(mesh):
    both = P(("emb", "seq"))
    rows = P(("emb", "seq"), None)
    return jax.shard_map(
        on_device,
        mesh=mesh,
        in_specs=(P("emb", None), P("emb", "seq", None, None), both, rows, P(), P(), rows),
        out_specs=(rows, rows, P(), P()),
        check_vma=False,
    )
```

time: 345 us -> 122 us (0.35); the launches traced: 340 us -> 121 us
  Pallas kernels: 0 us -> 114 us
  matrix products: 73.5 us -> 0 us
  local copies, waits for them, and re-layouts: 77.1 us -> 6.51 us
  other arithmetic: 59.5 us -> 0.05 us
  blocking collectives: 58.5 us -> 0 us
  waiting for transfers between devices: 46.7 us -> 0 us
  between operations: 16 us -> 0.85 us
  starting transfers between devices: 8.68 us -> 0 us
    pallas_call x0 -> x4, Pallas kernels: none -> 114 us  [the longest x1 46 us: share_grads(): pl.pallas_call(functools.partial(share, n_emb, n_seq), name='share', out_...]
    dot_general x12 -> x0, matrix products: 73.5 us -> none  [the longest x3 24.7 us: hstu_layer(): jnp.einsum('ihd,jhd->hij', queries, key_rows, preferred_element_type=jnp....]
    all_to_all x2 -> x0, blocking collectives: 58.5 us -> none  [the longest x1 42.3 us: in_one_piece(): lax.all_to_all(both, axis, split_axis=split_dim, concat_axis=concat_dim,...]
    unnamed x42 -> x8, local copies, waits for them, and re-layouts: 37.8 us -> 5.75 us
    all_gather x1 -> x0, waiting for transfers between devices: 22.7 us -> none  [in_one_piece_2(): out, at, done = (lax.all_gather(both, axis, axis=dim, tiled=True), 0, [])]
    reshape x8 -> x0, local copies, waits for them, and re-layouts: 21.5 us -> none  [the longest x1 5.25 us: on_device(): in_total = whole_first.reshape(first_grad.shape)]
    all_to_all x2 -> x0, waiting for transfers between devices: 20.4 us -> none  [the longest x1 10.8 us: on_device(): lax.all_to_all(slot_grad.reshape(emb_count, -1, model_width).astype(jnp.b...]
    scatter-add x2 -> x0, other arithmetic: 17.1 us -> none  [the longest x1 9.09 us: on_device(): jax.ops.segment_sum(row_grad.astype(jnp.float32), event_slot, num_segment...]
  transfers between devices with their start and end apart: 4 -> 0, of which waited for: 4 -> 0; matrix products, arithmetic and copies ran while one was open for 15% -> 0% of each run, Pallas kernels for 0% -> 0%
where the time goes in v1:
time: 122 us; the launch traced here: 121 us
  Pallas kernels  114 us (93%)
  local copies, waits for them, and re-layouts  6.51 us (5%)
    pallas_call x1, Pallas kernels, share_grads(): pl.pallas_call(functools.partial(share, n_emb, n_seq), name='share', out_...  46 us
    pallas_call x1, Pallas kernels, local_layer(): pl.pallas_call(compute, name='layer', out_shape=(jax.ShapeDtypeStruct((to...  40.2 us
    pallas_call x1, Pallas kernels, fetch_rows_of(): pl.pallas_call(functools.partial(fetch, n_emb, n_seq), name='fetch', out_...  22.9 us
    unnamed x8, local copies, waits for them, and re-layouts  5.75 us
    pallas_call x1, Pallas kernels, finish_grads(): pl.pallas_call(functools.partial(finish, n_seq), name='finish', out_shape...  4.7 us

profile of v1, /device:TPU:1, one launch (start us, length us, event | category | flops | bytes accessed | tf_op | source)
XLA Modules:
  0.0 121.3 jit_solution(16376046023533688853)
XLA Ops:
  0.7 0.7 tile.11
  1.4 0.1 copy.12
  1.5 0.0 copy-start
  1.5 2.2 %copy-done = bf16[4096,512]{1,0:T(8,128)(2,1)S(1)} copy-done((bf16[4096,512]{1,0:T(8,128)(2,1)S(1)}, bf16[4096,512]{1,0:T(8,128)(2,1)}, u32[]{:S(2)}) %copy-start) | copy-done | bytes 4194328
  3.7 22.9 %fetch.1 = (bf16[512,512]{1,0:T(8,128)(2,1)S(1)}, s32[4,32,1,128]{3,2,1,0:T(1,128)S(1)}) custom-call(s32[32,1,128]{2,1,0:T(1,128)S(1)} %compare_select_fusion.req_ref, bf16[4096,512]{1,0:T(8,128)(2,1)S(1)} %copy-done), custom_call_target="tpu_custom_call" | custom-call | tf_op jit(solution)/shard_map/fetch/pallas_call | solution.py:341
  26.6 0.0 copy-start.3
  26.6 0.8 copy-done.3
  27.4 40.2 %layer.1 = (bf16[1024,512]{1,0:T(8,128)(2,1)}, bf16[512,512]{1,0:T(8,128)(2,1)}, bf16[640,16,128]{2,1,0:T(8,128)(2,1)}) custom-call(s32[1,8]{1,0:T(1,128)} %len_ref.1, s32[8,128]{1,0:T(8,128)} %bitcast.5, bf16[512,512]{1,0:T(8,128)(2,1)} %copy-done.3, bf16[512,2048]{1,0:T(8,128)(2,1)} %win_ref.1, bf16[512,512]{1,0:T(8,128)(2,1)} %wout_ref.1, ...), custom_call_target="tpu_custom_call" | custom-call | flops 14000000000 | bytes 8000000 | tf_op jit(solution)/shard_map/layer/pallas_call | solution.py:239
  67.6 0.0 copy-start.1
  67.6 1.7 %copy-done.1 = bf16[640,16,128]{2,1,0:T(8,128)(2,1)S(1)} copy-done((bf16[640,16,128]{2,1,0:T(8,128)(2,1)S(1)}, bf16[640,16,128]{2,1,0:T(8,128)(2,1)}, u32[]{:S(2)}) %copy-start.1) | copy-done | bytes 2621464
  69.4 0.0 copy-start.2
  69.4 1.0 copy-done.2
  70.4 46.0 %share.1 = (bf16[4,512,512]{2,1,0:T(8,128)(2,1)S(1)}, bf16[640,16,128]{2,1,0:T(8,128)(2,1)S(1)}) custom-call(bf16[512,512]{1,0:T(8,128)(2,1)S(1)} %copy-done.2, bf16[640,16,128]{2,1,0:T(8,128)(2,1)S(1)} %copy-done.1), custom_call_target="tpu_custom_call" | custom-call | tf_op jit(solution)/shard_map/share/pallas_call | solution.py:549
  116.4 4.7 %finish.1 = (f32[1024,512]{1,0:T(8,128)}, f32[512,2048]{1,0:T(8,128)}, f32[512,512]{1,0:T(8,128)}) custom-call(s32[4,32,1,128]{3,2,1,0:T(1,128)S(1)} %get-tuple-element.16.idx_ref, bf16[4,512,512]{2,1,0:T(8,128)(2,1)S(1)} %get-tuple-element.19.all_ref, bf16[640,16,128]{2,1,0:T(8,128)(2,1)S(1)} %get-tuple-element.20.sum_ref), custom_call_target="tpu_custom_call" | custom-call | tf_op jit(solution)/shard_map/finish/pallas_call | solution.py:614
  (3 shorter events, 0.0 us)
Async XLA Ops:
  1.5 2.2 %copy-start = (bf16[4096,512]{1,0:T(8,128)(2,1)S(1)}, bf16[4096,512]{1,0:T(8,128)(2,1)}, u32[]{:S(2)}) copy-start(bf16[4096,512]{1,0:T(8,128)(2,1)} %table_ref.1) | copy-start | bytes 12582916
  26.6 0.8 copy-start.3
  67.6 1.7 %copy-start.1 = (bf16[640,16,128]{2,1,0:T(8,128)(2,1)S(1)}, bf16[640,16,128]{2,1,0:T(8,128)(2,1)}, u32[]{:S(2)}) copy-start(bf16[640,16,128]{2,1,0:T(8,128)(2,1)} %get-tuple-element.18.g_ref) | copy-start | bytes 7864324
  69.4 1.0 copy-start.2

commit v2 on v0

v2 whole, which is shorter than its diff:
```python
import functools, math
import jax, jax.numpy as jnp
from jax import lax
from jax.experimental import pallas as pl
from jax.experimental.pallas import tpu as pltpu
from jax.sharding import PartitionSpec as P

F32, BF16 = jnp.float32, jnp.bfloat16
EPS = 1e-05
MOST = 512
B = 256
LAST = (((1,), (1,)), ((), ()))


def rows_at(i):
    return pl.ds(pl.multiple_of(i * B, B), B)


def expand(ev_ref, tab_ref, events_s, pick_s):
    slots = tab_ref.shape[0]
    ev = ev_ref[...]
    ev_t = jnp.transpose(ev)
    lane = lax.broadcasted_iota(jnp.int32, (128, slots), 1)
    sub = lax.broadcasted_iota(jnp.int32, (slots, 128), 0)
    for a in range(ev.shape[0]):
        hot = jnp.where(ev_t[:, a : a + 1] == lane, 1.0, 0.0).astype(BF16)
        events_s[128 * a : 128 * a + 128, :] = jnp.dot(
            hot, tab_ref[...], preferred_element_type=F32
        ).astype(BF16)
        pick_s[:, 128 * a : 128 * a + 128] = jnp.where(sub == ev[a : a + 1, :], 1.0, 0.0).astype(
            BF16
        )


def project(r, events_s, win_ref, normed_s, normed_t, rstd_s, gate_s, dsil_s, qkv_s, kv_t):
    rows = rows_at(r)
    width = events_s.shape[1]
    e = events_s[rows, :].astype(F32)
    c = e - jnp.mean(e, axis=-1, keepdims=True)
    rs = lax.rsqrt(jnp.mean(c * c, axis=-1, keepdims=True) + EPS)
    n = (c * rs).astype(BF16)
    normed_s[rows, :] = n
    rstd_s[rows, :] = rs
    normed_t[:, rows] = jnp.transpose(n)
    for b in range(4):
        cols = slice(b * width, (b + 1) * width)
        x = jnp.dot(n, win_ref[:, cols], preferred_element_type=F32)
        hx = 0.5 * x
        t = jnp.tanh(hx)
        u = 1.0 + t
        y = hx * u
        dsil_s[rows, cols] = (0.5 * (u + hx * (1.0 - t * t))).astype(BF16)
        if b == 0:
            gate_s[rows, :] = y
        else:
            yb = y.astype(BF16)
            qkv_s[b - 1, rows, :] = yb
            if b == 1:
                kv_t[1, :, rows] = jnp.transpose(yb)
            elif b == 3:
                kv_t[0, :, rows] = jnp.transpose(yb)


def pairs(blocks):
    back = MOST // B
    return [(q, k) for q in range(blocks) for k in range(max(0, q - back), q + 1)]


def attend(h, starts, qkv_s, kv_t, att_t, p_s, d_s, blocks):
    hc = pl.ds(pl.multiple_of(h * 128, 128), 128)
    lane = lax.broadcasted_iota(jnp.int32, (B, B), 1)
    sub = lax.broadcasted_iota(jnp.int32, (B, B), 0)
    head = 128
    c1 = 0.5 / math.sqrt(head)
    total = None
    for i, (q, k) in enumerate(pairs(blocks)):
        kk = qkv_s[2, k * B : (k + 1) * B, hc]
        qq = qkv_s[1, q * B : (q + 1) * B, hc]
        x = lax.dot_general(kk, qq, LAST, preferred_element_type=F32)
        hh = x * c1
        t = jnp.tanh(hh)
        u = 1.0 + t
        mask = (sub + k * B) >= starts[q]
        if q == k:
            mask = mask & (sub <= lane)
        w = jnp.where(mask, (hh * u) * (1.0 / MOST), 0.0).astype(BF16)
        d = jnp.where(mask, (u + hh * (1.0 - t * t)) * (c1 / MOST), 0.0).astype(BF16)
        p_s[h, i] = w
        d_s[h, i] = d
        o = jnp.dot(kv_t[1, hc, k * B : (k + 1) * B], w, preferred_element_type=F32)
        total = o if k == max(0, q - MOST // B) else total + o
        if q == k:
            att_t[hc, q * B : (q + 1) * B] = total


def middle(r, att_t, gate_s, dsil_s, events_s, wout_ref, og_ref, lo_ref, gated_t, dx_s, do_s):
    rows = rows_at(r)
    width = events_s.shape[1]
    a = jnp.transpose(att_t[:, rows])
    c = a - jnp.mean(a, axis=-1, keepdims=True)
    rs = lax.rsqrt(jnp.mean(c * c, axis=-1, keepdims=True) + EPS)
    xh = c * rs
    gate = gate_s[rows, :]
    gated = (xh * gate).astype(BF16)
    out = jnp.dot(gated, wout_ref[...], preferred_element_type=F32)
    lo_ref[rows, :] = (out + events_s[rows, :].astype(F32)).astype(BF16)
    gated_t[:, rows] = jnp.transpose(gated)
    og = og_ref[rows, :]
    dg = lax.dot_general(og, wout_ref[...], LAST, preferred_element_type=F32)
    dg = dg.astype(BF16).astype(F32)
    dx_s[rows, :width] = (dg * xh * dsil_s[rows, :width].astype(F32)).astype(BF16)
    dxh = dg * gate
    m1 = jnp.mean(dxh, axis=-1, keepdims=True)
    m2 = jnp.mean(dxh * xh, axis=-1, keepdims=True)
    do_s[rows, :] = (rs * (dxh - m1 - xh * m2)).astype(BF16)


def attend_back(h, qkv_s, kv_t, p_s, d_s, do_s, dsil_s, dx_s, dq_t, blocks, width):
    hc = slice(h * 128, (h + 1) * 128)

    def put(block, part, grad):
        cols = slice(part * width + h * 128, part * width + (h + 1) * 128)
        rows = slice(block * B, (block + 1) * B)
        dx_s[rows, cols] = (
            grad.astype(BF16).astype(F32) * dsil_s[rows, cols].astype(F32)
        ).astype(BF16)

    order = pairs(blocks)
    for k in range(blocks):
        dv = dk = None
        vv = qkv_s[0, k * B : (k + 1) * B, hc]
        for q in range(k, min(k + MOST // B, blocks - 1) + 1):
            i = order.index((q, k))
            do = do_s[q * B : (q + 1) * B, hc]
            dp = lax.dot_general(vv, do, LAST, preferred_element_type=F32).astype(BF16)
            ds = dp * d_s[h, i]
            dv1 = jnp.dot(p_s[h, i], do, preferred_element_type=F32)
            dk1 = jnp.dot(ds, qkv_s[1, q * B : (q + 1) * B, hc], preferred_element_type=F32)
            dv = dv1 if dv is None else dv + dv1
            dk = dk1 if dk is None else dk + dk1
            dq1 = jnp.dot(kv_t[0, hc, k * B : (k + 1) * B], ds, preferred_element_type=F32)
            at = slice(q * B, (q + 1) * B)
            if k == max(0, q - MOST // B):
                dq_t[:, at] = dq1
            else:
                dq_t[:, at] += dq1
        put(k, 1, dv)
        put(k, 3, dk)
    for q in range(blocks):
        put(q, 2, jnp.transpose(dq_t[:, q * B : (q + 1) * B]))


def event_back(r, dx_s, win_ref, normed_s, rstd_s, og_ref, eg_s):
    rows = rows_at(r)
    g = lax.dot_general(dx_s[rows, :], win_ref[...], LAST, preferred_element_type=F32)
    g = g.astype(BF16).astype(F32)
    xh = normed_s[rows, :].astype(F32)
    m1 = jnp.mean(g, axis=-1, keepdims=True)
    m2 = jnp.mean(g * xh, axis=-1, keepdims=True)
    de = (rstd_s[rows, :] * (g - m1 - xh * m2)).astype(BF16)
    eg_s[rows, :] = (de.astype(F32) + og_ref[rows, :].astype(F32)).astype(BF16)


def row_starts(len_ref, blocks):
    ends, at = [], jnp.int32(0)
    for s in range(len_ref.shape[1]):
        at = at + len_ref[0, s]
        ends.append(at)
    starts = []
    for q in range(blocks):
        place = lax.broadcasted_iota(jnp.int32, (1, B), 1) + q * B
        start = jnp.zeros((1, B), jnp.int32)
        for e in ends:
            start = jnp.where(place >= e, e, start)
        starts.append(start)
    return starts


def compute_scratch(tokens, width, slots):
    n = len(pairs(tokens // B))
    heads = width // 128
    return [
        pltpu.VMEM((tokens, width), BF16),
        pltpu.VMEM((slots, tokens), BF16),
        pltpu.VMEM((tokens, width), BF16),
        pltpu.VMEM((width, tokens), BF16),
        pltpu.VMEM((tokens, 1), F32),
        pltpu.VMEM((tokens, width), F32),
        pltpu.VMEM((tokens, 4 * width), BF16),
        pltpu.VMEM((3, tokens, width), BF16),
        pltpu.VMEM((2, width, tokens), BF16),
        pltpu.VMEM((width, tokens), F32),
        pltpu.VMEM((heads, n, B, B), BF16),
        pltpu.VMEM((heads, n, B, B), BF16),
        pltpu.VMEM((width, tokens), BF16),
        pltpu.VMEM((tokens, 4 * width), BF16),
        pltpu.VMEM((tokens, width), BF16),
        pltpu.VMEM((128, tokens), F32),
        pltpu.VMEM((tokens, width), BF16),
    ]


MESH = pl.DeviceIdType.MESH


def remote(src, dst, send_sem, recv_sem, emb, seq):
    return pltpu.make_async_remote_copy(
        src_ref=src, dst_ref=dst, send_sem=send_sem, recv_sem=recv_sem,
        device_id=(emb, seq), device_id_type=MESH,
    )


def rows_of(at, count):
    return pl.ds(pl.multiple_of(at * count, count), count)


def greet(peers):
    barrier = pltpu.get_barrier_semaphore()
    for emb, seq in peers:
        pl.semaphore_signal(barrier, inc=1, device_id=(emb, seq), device_id_type=MESH)
    pl.semaphore_wait(barrier, len(peers))


class Summed:
    def __init__(self, e, s, base, units, g_s, sum_s, bufs, sems):
        self.e, self.s = e, s
        self.c, self.x, self.z = lax.rem(e, 2), lax.rem(e // 2, 4), e // 8
        self.chip = e // 2
        self.other = e + 1 - 2 * self.c
        self.base, self.half, self.piece = base, units // 2, units // 32
        self.g_s, self.sum_s = g_s, sum_s
        self.half_s, self.pair_s, self.b1, self.b3 = bufs
        self.many_send, self.many_recv, self.few_send, self.few_recv = sems

    def chips(self, t):
        z = lax.rem(self.z + t, 4)
        return [z * 4 + lax.rem(self.x + u, 4) for u in range(0 if t else 1, 4)]

    def line(self, t):
        return lax.rem(self.z + t, 4) * 4 * self.piece

    def halve(self, t):
        src = self.g_s.at[pl.ds(self.base + (1 - self.c) * self.half + self.line(t), 4 * self.piece)]
        dst = self.pair_s.at[pl.ds(self.line(t), 4 * self.piece)]
        return remote(src, dst, self.few_send.at[0, t], self.few_recv.at[0, t], self.other, self.s)

    def spread(self, to):
        return remote(self.half_s.at[pl.ds(to * self.piece, self.piece)], self.b1.at[self.chip],
                      self.many_send.at[0, to], self.many_recv.at[0, self.chip],
                      to * 2 + self.c, self.s)

    def spread_from(self, frm):
        return remote(self.half_s.at[pl.ds(0, self.piece)], self.b1.at[frm],
                      self.many_send.at[0, frm], self.many_recv.at[0, frm],
                      frm * 2 + self.c, self.s)

    def gather3(self, d):
        ref = self.b3.at[self.s]
        return remote(ref, ref, self.few_send.at[1, d], self.few_recv.at[1, d],
                      self.e, lax.rem(self.s + d, 4))

    def own(self, chip):
        return self.sum_s.at[pl.ds(self.base + self.c * self.half + chip * self.piece, self.piece)]

    def back(self, to):
        return remote(self.own(self.chip), self.own(self.chip),
                      self.many_send.at[1, to], self.many_recv.at[1, self.chip],
                      to * 2 + self.c, self.s)

    def back_from(self, frm):
        return remote(self.own(frm), self.own(frm),
                      self.many_send.at[1, frm], self.many_recv.at[1, frm],
                      frm * 2 + self.c, self.s)

    def join(self, t):
        ref = self.sum_s.at[pl.ds(self.base + self.c * self.half + self.line(t), 4 * self.piece)]
        return remote(ref, ref, self.few_send.at[2, t], self.few_recv.at[2, t], self.other, self.s)

    def step0(self):
        for t in (2, 1, 3, 0):
            self.halve(t).start()

    def step1(self):
        for t in (2, 1, 3, 0):
            self.halve(t).wait_recv()
            part = pl.ds(self.line(t), 4 * self.piece)
            mine = self.g_s[pl.ds(self.base + self.c * self.half + self.line(t), 4 * self.piece)]
            self.half_s[part] = (mine.astype(F32) + self.pair_s[part].astype(F32)).astype(BF16)
            for to in self.chips(t):
                self.spread(to).start()

    def step2(self):
        total = self.half_s[pl.ds(self.chip * self.piece, self.piece)].astype(F32)
        for t in range(4):
            for frm in self.chips(t):
                self.spread_from(frm).wait_recv()
        for t in range(4):
            for frm in self.chips(t):
                total = total + self.b1[frm].astype(F32)
        self.b3[self.s] = total.astype(BF16)
        for d in (2, 1, 3):
            self.gather3(d).start()

    def step3(self):
        for d in range(1, 4):
            self.gather3(d).wait_recv()
        total = self.b3[0].astype(F32)
        for j in range(1, 4):
            total = total + self.b3[j].astype(F32)
        self.own(self.chip)[...] = total.astype(BF16)
        for t in (2, 1, 3, 0):
            for to in self.chips(t):
                self.back(to).start()

    def step4(self):
        for t in (0, 1, 3, 2):
            for frm in self.chips(t):
                self.back_from(frm).wait_recv()
            self.join(t).start()

    def step5(self):
        for t in range(4):
            self.join(t).wait_recv()

    def drain(self):
        for t in range(4):
            self.halve(t).wait_send()
            self.join(t).wait_send()
            for to in self.chips(t):
                self.spread(to).wait_send()
                self.back(to).wait_send()
        for d in range(1, 4):
            self.gather3(d).wait_send()


PARTS = (256, 192, 192)


def whole(n_emb, n_seq, len_ref, asked_ref, ev_ref, table_ref, win_ref, wout_ref, og_ref,
          lo_ref, tg_ref, total_ref,
          idx_ref, tgb_s, req_ref, table_v, rows_v, tab_s, win_s, wout_s, og_s, lo_s, g_s, sum_s, sg_s, all_s,
          bufs_e, bufs_m, bufs_l, load, save, i_send, i_recv, j_send, j_recv, r_send, r_recv, g_send, g_recv,
          y_send, y_recv, z_send, z_recv, many_send, many_recv, few_send, few_recv,
          events_s, pick_s, normed_s, normed_t, rstd_s, gate_s, dsil_s, qkv_s, kv_t,
          att_t, p_s, d_s, gated_t, dx_s, do_s, dq_t, eg_s):
    e, s = lax.axis_index("emb"), lax.axis_index("seq")
    tokens, width = og_s.shape
    blocks, heads = tokens // B, width // 128
    cap = tab_s.shape[0] // n_emb
    per = 128 // cap
    groups = n_emb // per
    mine, inner = e // per, lax.rem(e, per)
    loads = [pltpu.make_async_copy(a, b, load.at[i]) for i, (a, b) in enumerate(
        ((table_ref, table_v), (win_ref, win_s), (og_ref, og_s), (wout_ref, wout_s)))]
    for copy in loads:
        copy.start()
    greet([(lax.rem(e + d, n_emb), s) for d in range(1, n_emb)]
          + [(e, lax.rem(s + d, n_seq)) for d in range(1, n_seq)])

    def members(j):
        g = lax.rem(mine + j, groups)
        first = 1 if j == 0 else 0
        return g, [g * per + lax.rem(inner + t, per) for t in range(first, per)]

    def ask(to):
        return remote(req_ref.at[to], idx_ref.at[s, e], i_send.at[to], i_recv.at[e], to, s)

    def asked(frm):
        return remote(req_ref.at[frm], idx_ref.at[s, frm], i_send.at[frm], i_recv.at[frm], frm, s)

    rows_asked = asked_ref[0, 0]
    spot = jnp.where(lax.broadcasted_iota(jnp.int32, (cap, 128), 1)
                     == lax.broadcasted_iota(jnp.int32, (cap, 128), 0) + cap * inner, 1.0, 0.0)
    low = rows_asked & 127
    high = (rows_asked - low).astype(F32)
    spread_out = (jnp.dot(high.astype(BF16), spot.astype(BF16), preferred_element_type=F32)
                  + jnp.dot(low.astype(F32).astype(BF16), spot.astype(BF16),
                            preferred_element_type=F32)).astype(jnp.int32)
    for to in range(n_emb):
        req_ref[to] = spread_out[to : to + 1, :]
    for j in (2, 1, 3, 0):
        for to in members(j)[1]:
            ask(to).start()
    idx_ref[s, e] = req_ref[e]
    shard = table_v.shape[0]
    lane = lax.broadcasted_iota(jnp.int32, (128, shard), 1)

    def answer(to, j):
        return remote(rows_v.at[j, rows_of(lax.rem(to, per), cap)], tab_s.at[rows_of(e, cap)],
                      r_send.at[to], r_recv.at[e], to, s)

    def answered(frm, j):
        return remote(rows_v.at[j, rows_of(lax.rem(frm, per), cap)], tab_s.at[rows_of(frm, cap)],
                      r_send.at[frm], r_recv.at[frm], frm, s)

    loads[0].wait()
    for j in (0, 1, 3, 2):
        g, them = members(j)
        for frm in them:
            asked(frm).wait_recv()
        row = idx_ref[s, g * per]
        for i in range(1, per):
            row = row + idx_ref[s, g * per + i]
        col = jnp.transpose(jnp.broadcast_to(row, (8, 128)))[:, 0:1]
        hot = jnp.where(col == lane, 1.0, 0.0).astype(BF16)
        rows_v[j] = jnp.dot(hot, table_v[...], preferred_element_type=F32).astype(BF16)
        for to in them:
            answer(to, j).start()
        if j == 0:
            tab_s[rows_of(e, cap), :] = rows_v[0, rows_of(inner, cap), :]

    def tell(d):
        to = lax.rem(s + d, n_seq)
        return remote(idx_ref.at[s], idx_ref.at[s], j_send.at[d], j_recv.at[d], e, to)

    for d in range(1, n_seq):
        tell(d).start()
    for j in range(groups):
        for frm in members(j)[1]:
            answered(frm, j).wait_recv()
    for copy in loads[1:]:
        copy.wait()

    expand(ev_ref, tab_s, events_s, pick_s)
    pl.loop(0, blocks)(lambda r: project(
        r, events_s, win_s, normed_s, normed_t, rstd_s, gate_s, dsil_s, qkv_s, kv_t))
    starts = row_starts(len_ref, blocks)
    pl.loop(0, heads)(lambda h: attend(h, starts, qkv_s, kv_t, att_t, p_s, d_s, blocks))
    pl.loop(0, blocks)(lambda r: middle(
        r, att_t, gate_s, dsil_s, events_s, wout_s, og_s, lo_s, gated_t, dx_s, do_s))
    saves = [pltpu.make_async_copy(lo_s, lo_ref, save.at[0])]
    saves[0].start()

    def put_grad(c, val):
        g_s[pl.ds(c * 64, 32)] = val[:, :128].astype(BF16).reshape(32, 16, 128)
        g_s[pl.ds(c * 64 + 32, 32)] = val[:, 128:].astype(BF16).reshape(32, 16, 128)

    for c in range(2):
        put_grad(c, jnp.dot(normed_t[...], dx_s[:, c * B : (c + 1) * B],
                            preferred_element_type=F32))
        put_grad(2 + c, jnp.dot(gated_t[...], og_s[:, c * B : (c + 1) * B],
                                preferred_element_type=F32))
    sums, base = [], 0
    for i, (units, bufs) in enumerate(zip(PARTS, (bufs_e, bufs_m, bufs_l))):
        sems = [sem.at[i] for sem in (many_send, many_recv, few_send, few_recv)]
        sums.append(Summed(e, s, base, units, g_s, sum_s, bufs, sems))
        base += units
    early, mid, late = sums
    early.step0()

    def back(h):
        attend_back(h, qkv_s, kv_t, p_s, d_s, do_s, dsil_s, dx_s, dq_t, blocks, width)

    def grads_of(c):
        for b in range(3):
            cols = slice((b + 1) * width + c * B, (b + 1) * width + (c + 1) * B)
            put_grad(4 + 3 * c + b, jnp.dot(normed_t[...], dx_s[:, cols],
                                            preferred_element_type=F32))

    back(0)
    early.step1()
    back(1)
    grads_of(0)
    mid.step0()
    back(2)
    mid.step1()
    back(3)
    early.step2()
    pl.loop(0, blocks)(lambda r: event_back(r, dx_s, win_s, normed_s, rstd_s, og_s, eg_s))
    early.step3()
    sg_s[...] = jnp.dot(pick_s[...], eg_s[...], preferred_element_type=F32).astype(BF16)

    def give(to):
        return remote(sg_s.at[rows_of(to, cap)], all_s.at[s, rows_of(e, cap)],
                      g_send.at[to], g_recv.at[e], to, s)

    def given(frm):
        return remote(sg_s.at[rows_of(frm, cap)], all_s.at[s, rows_of(frm, cap)],
                      g_send.at[frm], g_recv.at[frm], frm, s)

    for j in (0, 1, 3, 2):
        for to in members(j)[1]:
            give(to).start()
    all_s[s, rows_of(e, cap), :] = sg_s[rows_of(e, cap), :]
    grads_of(1)
    late.step0()
    mid.step2()
    chunk = all_s.shape[1] // groups
    up, down = lax.rem(s + 1, n_seq), lax.rem(s + n_seq - 1, n_seq)

    def pass_on(j, way):
        ref = all_s.at[s, rows_of(lax.rem(mine + j, groups), chunk)]
        return remote(ref, ref, y_send.at[way, j], y_recv.at[way, j], e, down if way else up)

    def relay(j):
        frm, to = (down, up) if j % 2 else (up, down)
        ref = all_s.at[frm, rows_of(lax.rem(mine + j, groups), chunk)]
        return remote(ref, ref, z_send.at[j], z_recv.at[j], e, to)

    def arrived(j):
        for frm in members(j)[1]:
            given(frm).wait_recv()
        for way in range(2):
            pass_on(j, way).start()

    def further(j):
        pass_on(j, 0 if j % 2 else 1).wait_recv()
        relay(j).start()

    def keep(i):
        rows = pl.ds(sums[i].base, PARTS[i])
        saves.append(pltpu.make_async_copy(sum_s.at[rows], total_ref.at[rows], save.at[2 + i]))
        saves[-1].start()

    part = gate_s.shape[0]
    sub = lax.broadcasted_iota(jnp.int32, (part, 128), 0) + s * part
    for d in range(1, n_seq):
        tell(d).wait_recv()
    for n in range(n_seq):
        for j in range(groups):
            g = lax.rem(mine + j, groups)
            frm = lax.rem(s + n, n_seq)
            row = idx_ref[frm, g * per]
            for i in range(1, per):
                row = row + idx_ref[frm, g * per + i]
            at = (n * groups + j) * 128
            dsil_s[:, at : at + 128] = jnp.where(sub == row, 1.0, 0.0).astype(BF16)

    def add(n, js):
        frm = lax.rem(s + n, n_seq)
        rows = jnp.concatenate(
            [all_s[frm, rows_of(lax.rem(mine + j, groups), chunk), :] for j in js], axis=0)
        at = (n * groups + js[0]) * 128

        @pl.loop(0, blocks)
        def _(r):
            val = jnp.dot(dsil_s[rows_at(r), at : at + 256], rows, preferred_element_type=F32)
            if n == 0 and js[0] == 0:
                gate_s[rows_at(r), :] = val
            else:
                gate_s[rows_at(r), :] += val

    def keep(i):
        rows = pl.ds(sums[i].base, PARTS[i])
        saves.append(pltpu.make_async_copy(sum_s.at[rows], total_ref.at[rows], save.at[2 + i]))
        saves[-1].start()

    arrived(0)
    late.step1()
    arrived(1)
    mid.step3()
    early.step4()
    further(0)
    add(0, (0, 1))
    arrived(2)
    late.step2()
    further(1)
    arrived(3)
    mid.step4()
    add(0, (2, 3))
    late.step3()
    further(2)
    early.step5()
    keep(0)
    for way in range(2):
        for j in (0, 1):
            if way != (0 if j % 2 else 1):
                pass_on(j, way).wait_recv()
    add(1, (0, 1))
    add(3, (0, 1))
    further(3)
    mid.step5()
    keep(1)
    late.step4()
    for way in range(2):
        for j in (2, 3):
            if way != (0 if j % 2 else 1):
                pass_on(j, way).wait_recv()
    add(1, (2, 3))
    add(3, (2, 3))
    relay(0).wait_recv()
    relay(1).wait_recv()
    add(2, (0, 1))
    late.step5()
    keep(2)
    relay(2).wait_recv()
    relay(3).wait_recv()
    add(2, (2, 3))
    tgb_s[...] = gate_s[...].astype(BF16)
    saves.append(pltpu.make_async_copy(tgb_s, tg_ref, save.at[1]))
    saves[-1].start()
    for d in range(1, n_seq):
        tell(d).wait_send()
    for j in range(groups):
        for to in members(j)[1]:
            ask(to).wait_send()
            answer(to, j).wait_send()
            give(to).wait_send()
        relay(j).wait_send()
        for way in range(2):
            pass_on(j, way).wait_send()
    for part in sums:
        part.drain()
    for copy in saves:
        copy.wait()


def layer_grads(lengths, asked, ev, table, win, wout, og, n_emb, n_seq, slots):
    vm = pl.BlockSpec(memory_space=pltpu.VMEM)
    hbm = pl.BlockSpec(memory_space=pl.ANY)
    tokens, width = og.shape
    tile = (16, 128)
    units = 5 * width * width // (16 * 128)
    dma = pltpu.SemaphoreType.DMA

    def sums(n):
        shapes = [(n // 2,), (n // 2,), (16, n // 32), (n_seq, n // 32)]
        return tuple(pltpu.VMEM(shape + tile, BF16) for shape in shapes)

    return pl.pallas_call(
        functools.partial(whole, n_emb, n_seq),
        name="layer",
        out_shape=(
            jax.ShapeDtypeStruct((tokens, width), BF16),
            jax.ShapeDtypeStruct((tokens, width), BF16),
            jax.ShapeDtypeStruct((units,) + tile, BF16),
        ),
        in_specs=[pl.BlockSpec(memory_space=pltpu.SMEM), vm, vm] + [hbm] * 4,
        out_specs=(hbm, hbm, hbm),
        scratch_shapes=[
            pltpu.VMEM((n_seq, n_emb, 1, 128), jnp.int32),
            pltpu.VMEM((tokens, width), BF16),
            pltpu.VMEM((n_emb, 1, 128), jnp.int32),
            pltpu.VMEM(table.shape, BF16),
            pltpu.VMEM((4, 128, width), BF16),
            pltpu.VMEM((slots, width), BF16),
            pltpu.VMEM(win.shape, BF16),
            pltpu.VMEM(wout.shape, BF16),
            pltpu.VMEM(og.shape, BF16),
            pltpu.VMEM(og.shape, BF16),
            pltpu.VMEM((units,) + tile, BF16),
            pltpu.VMEM((units,) + tile, BF16),
            pltpu.VMEM((slots, width), BF16),
            pltpu.VMEM((n_seq, slots, width), BF16),
        ] + [sums(n) for n in PARTS] + [
            dma((4,)), dma((5,)),
            dma((n_emb,)), dma((n_emb,)), dma((n_seq,)), dma((n_seq,)),
            dma((n_emb,)), dma((n_emb,)), dma((n_emb,)), dma((n_emb,)),
            dma((2, 4)), dma((2, 4)), dma((4,)), dma((4,)),
            dma((3, 2, 16)), dma((3, 2, 16)), dma((3, 3, 4)), dma((3, 3, 4)),
        ] + compute_scratch(tokens, width, slots),
        compiler_params=pltpu.CompilerParams(
            collective_id=0, has_side_effects=True, vmem_limit_bytes=67043328),
    )(lengths, asked, ev, table, win, wout, og)


def finish(rows_ref, sum_ref, out_ref, tg_ref, wi_ref, wo_ref, lo_ref,
           rows_s, sum_s, lo_s, tg_v, wi_v, wo_v, load, sems):
    width = lo_s.shape[1]
    loads = [pltpu.make_async_copy(a, b, load.at[i]) for i, (a, b) in enumerate(
        ((rows_ref, rows_s), (sum_ref, sum_s), (out_ref, lo_s)))]
    for copy in loads:
        copy.start()
    loads[0].wait()
    tg_v[...] = rows_s[...].astype(F32)
    copies = [pltpu.make_async_copy(tg_v, tg_ref, sems.at[6])]
    copies[-1].start()
    loads[1].wait()
    tall = width // 4
    for r in range(4):
        for b in range(20):
            val = sum_s[b * 32 + r * 8 : b * 32 + r * 8 + 8].reshape(tall, 128).astype(F32)
            rows = slice(r * tall, (r + 1) * tall)
            if 4 <= b < 8:
                wo_v[rows, (b - 4) * 128 : (b - 3) * 128] = val
            else:
                half, part, head = (b - 8) // 6, (b - 8) % 6 // 2, b % 2
                at = b if b < 4 else 4 + part * 4 + half * 2 + head
                wi_v[rows, at * 128 : (at + 1) * 128] = val
        copies.append(pltpu.make_async_copy(wi_v.at[rows], wi_ref.at[rows], sems.at[r]))
        copies[-1].start()
    copies.append(pltpu.make_async_copy(wo_v, wo_ref, sems.at[4]))
    copies[-1].start()
    loads[2].wait()
    copies.append(pltpu.make_async_copy(lo_s, lo_ref, sems.at[5]))
    copies[-1].start()
    for copy in copies:
        copy.wait()


def finish_grads(rows, total, out):
    hbm = pl.BlockSpec(memory_space=pl.ANY)
    width = out.shape[1]
    shapes = [(rows.shape, F32), ((width, 4 * width), F32), ((width, width), F32)]
    return pl.pallas_call(
        finish,
        name="finish",
        out_shape=tuple(jax.ShapeDtypeStruct(*a) for a in shapes + [(out.shape, BF16)]),
        in_specs=[hbm] * 3,
        out_specs=(hbm,) * 4,
        scratch_shapes=[pltpu.VMEM(a.shape, BF16) for a in (rows, total, out)]
        + [pltpu.VMEM(*a) for a in shapes]
        + [pltpu.SemaphoreType.DMA((3,)), pltpu.SemaphoreType.DMA((7,))],
        compiler_params=pltpu.CompilerParams(vmem_limit_bytes=67043328),
    )(rows, total, out)


def on_device(item_table, fetch_rows, event_slot, lengths, in_weight, out_weight, out_grad):
    n_emb, n_seq = lax.axis_size("emb"), lax.axis_size("seq")
    cap = fetch_rows.shape[-1]
    layer_out, rows_grad, total = layer_grads(
        lengths, fetch_rows, event_slot.reshape(-1, 128), item_table,
        in_weight, out_weight, out_grad, n_emb, n_seq, n_emb * cap)
    table_grad, in_total, out_total, layer_out = finish_grads(rows_grad, total, layer_out)
    return layer_out, table_grad, in_total, out_total


def solution(mesh):
    both = P(("emb", "seq"))
    rows = P(("emb", "seq"), None)
    return jax.shard_map(
        on_device,
        mesh=mesh,
        in_specs=(P("emb", None), P("emb", "seq", None, None), both, rows, P(), P(), rows),
        out_specs=(rows, rows, P(), P()),
        check_vma=False,
    )
```

time: 345 us -> 107 us (0.31); the launches traced: 340 us -> 106 us
  Pallas kernels: 0 us -> 104 us
  local copies, waits for them, and re-layouts: 77.1 us -> 1.38 us
  matrix products: 73.5 us -> 0 us
  other arithmetic: 59.5 us -> 0 us
  blocking collectives: 58.5 us -> 0 us
  waiting for transfers between devices: 46.7 us -> 0 us
  between operations: 16 us -> 0.82 us
  starting transfers between devices: 8.68 us -> 0 us
    pallas_call x0 -> x2, Pallas kernels: none -> 104 us  [the longest x1 98.8 us: layer_grads(): pl.pallas_call(functools.partial(whole, n_emb, n_seq), name='layer', out_...]
    dot_general x12 -> x0, matrix products: 73.5 us -> none  [the longest x3 24.7 us: hstu_layer(): jnp.einsum('ihd,jhd->hij', queries, key_rows, preferred_element_type=jnp....]
    all_to_all x2 -> x0, blocking collectives: 58.5 us -> none  [the longest x1 42.3 us: in_one_piece(): lax.all_to_all(both, axis, split_axis=split_dim, concat_axis=concat_dim,...]
    unnamed x42 -> x1, local copies, waits for them, and re-layouts: 37.8 us -> 1.38 us
    all_gather x1 -> x0, waiting for transfers between devices: 22.7 us -> none  [in_one_piece_2(): out, at, done = (lax.all_gather(both, axis, axis=dim, tiled=True), 0, [])]
    reshape x8 -> x0, local copies, waits for them, and re-layouts: 21.5 us -> none  [the longest x1 5.25 us: on_device(): in_total = whole_first.reshape(first_grad.shape)]
    all_to_all x2 -> x0, waiting for transfers between devices: 20.4 us -> none  [the longest x1 10.8 us: on_device(): lax.all_to_all(slot_grad.reshape(emb_count, -1, model_width).astype(jnp.b...]
    scatter-add x2 -> x0, other arithmetic: 17.1 us -> none  [the longest x1 9.09 us: on_device(): jax.ops.segment_sum(row_grad.astype(jnp.float32), event_slot, num_segment...]
  transfers between devices with their start and end apart: 4 -> 0, of which waited for: 4 -> 0; matrix products, arithmetic and copies ran while one was open for 15% -> 0% of each run, Pallas kernels for 0% -> 0%
where the time goes in v2:
time: 107 us; the launch traced here: 106 us
  Pallas kernels  104 us (97%)
  local copies, waits for them, and re-layouts  1.38 us (1%)
    pallas_call x1, Pallas kernels, layer_grads(): pl.pallas_call(functools.partial(whole, n_emb, n_seq), name='layer', out_...  98.8 us
    pallas_call x1, Pallas kernels, finish_grads(): pl.pallas_call(finish, name='finish', out_shape=tuple((jax.ShapeDtypeStru...  4.86 us

profile of v2, /device:TPU:1, one launch (start us, length us, event | category | flops | bytes accessed | tf_op | source)
XLA Modules:
  0.0 105.9 jit_solution(9569663381302546726)
XLA Ops:
  0.6 1.4 %copy.11.asked_ref = s32[1,1,32,16]{3,2,1,0:T(8,128)} copy(s32[1,1,32,16]{2,3,1,0:T(8,128)} %param.8) | data formatting | bytes 4096 | tf_op args[1]
  2.0 98.8 %layer.1 = (bf16[1024,512]{1,0:T(8,128)(2,1)}, bf16[1024,512]{1,0:T(8,128)(2,1)}, bf16[640,16,128]{2,1,0:T(8,128)(2,1)}) custom-call(s32[1,8]{1,0:T(1,128)} %len_ref.1, s32[1,1,32,16]{3,2,1,0:T(8,128)} %copy.11.asked_ref, s32[8,128]{1,0:T(8,128)} %bitcast.1, bf16[4096,512]{1,0:T(8,128)(2,1)} %table_ref.1, bf16[512,2048]{1,0:T(8,128)(2,1)} %win_ref.1, ...), custom_call_target="tpu_custom_call" | custom-call | tf_op jit(solution)/shard_map/layer/pallas_call | solution.py:620
  100.9 4.9 %finish.1 = (f32[1024,512]{1,0:T(8,128)}, f32[512,2048]{1,0:T(8,128)}, f32[512,512]{1,0:T(8,128)}, bf16[1024,512]{1,0:T(8,128)(2,1)}) custom-call(bf16[1024,512]{1,0:T(8,128)(2,1)} %get-tuple-element.11.rows_ref, bf16[640,16,128]{2,1,0:T(8,128)(2,1)} %get-tuple-element.12.sum_ref, bf16[1024,512]{1,0:T(8,128)(2,1)} %get-tuple-element.13.out_ref), custom_call_target="tpu_custom_call" | custom-call | tf_op jit(solution)/shard_map/finish/pallas_call | solution.py:695

commit v3 on v2

--- a/solution.py
+++ b/solution.py
@@ -83,14 +83,14 @@
         mask = (sub + k * B) >= starts[q]
         if q == k:
             mask = mask & (sub <= lane)
-        w = jnp.where(mask, (hh * u) * (1.0 / MOST), 0.0).astype(BF16)
-        d = jnp.where(mask, (u + hh * (1.0 - t * t)) * (c1 / MOST), 0.0).astype(BF16)
+        w = jnp.where(mask, hh * u, 0.0).astype(BF16)
+        d = jnp.where(mask, u + hh * (1.0 - t * t), 0.0).astype(BF16)
         p_s[h, i] = w
         d_s[h, i] = d
         o = jnp.dot(kv_t[1, hc, k * B : (k + 1) * B], w, preferred_element_type=F32)
         total = o if k == max(0, q - MOST // B) else total + o
         if q == k:
-            att_t[hc, q * B : (q + 1) * B] = total
+            att_t[hc, q * B : (q + 1) * B] = total * (1.0 / MOST)
 
 
 def middle(r, att_t, gate_s, dsil_s, events_s, wout_ref, og_ref, lo_ref, gated_t, dx_s, do_s):
@@ -126,6 +126,7 @@
         ).astype(BF16)
 
     order = pairs(blocks)
+    scale = 0.5 / math.sqrt(128) / MOST
     for k in range(blocks):
         dv = dk = None
         vv = qkv_s[0, k * B : (k + 1) * B, hc]
@@ -144,10 +145,10 @@
                 dq_t[:, at] = dq1
             else:
                 dq_t[:, at] += dq1
-        put(k, 1, dv)
-        put(k, 3, dk)
+        put(k, 1, dv * (1.0 / MOST))
+        put(k, 3, dk * scale)
     for q in range(blocks):
-        put(q, 2, jnp.transpose(dq_t[:, q * B : (q + 1) * B]))
+        put(q, 2, jnp.transpose(dq_t[:, q * B : (q + 1) * B] * scale))
 
 
 def event_back(r, dx_s, win_ref, normed_s, rstd_s, og_ref, eg_s):
@@ -230,7 +231,8 @@
         self.base, self.half, self.piece = base, units // 2, units // 32
         self.g_s, self.sum_s = g_s, sum_s
         self.half_s, self.pair_s, self.b1, self.b3 = bufs
-        self.many_send, self.many_recv, self.few_send, self.few_recv = sems
+        (self.many_send, self.many_recv, self.few_send, self.few_recv,
+         self.wide_send, self.wide_recv) = sems
 
     def chips(self, t):
         z = lax.rem(self.z + t, 4)
@@ -259,18 +261,24 @@
         return remote(ref, ref, self.few_send.at[1, d], self.few_recv.at[1, d],
                       self.e, lax.rem(self.s + d, 4))
 
-    def own(self, chip):
-        return self.sum_s.at[pl.ds(self.base + self.c * self.half + chip * self.piece, self.piece)]
-
-    def back(self, to):
-        return remote(self.own(self.chip), self.own(self.chip),
-                      self.many_send.at[1, to], self.many_recv.at[1, self.chip],
-                      to * 2 + self.c, self.s)
-
-    def back_from(self, frm):
-        return remote(self.own(frm), self.own(frm),
-                      self.many_send.at[1, frm], self.many_recv.at[1, frm],
-                      frm * 2 + self.c, self.s)
+    def own(self, dz, dx, k):
+        chip = lax.rem(self.z + dz, 4) * 4 + lax.rem(self.x + dx, 4)
+        size = self.piece // 2
+        at = self.base + self.c * self.half + chip * self.piece + k * size
+        return self.sum_s.at[pl.ds(at, size)]
+
+    def chip_at(self, dz, dx):
+        return (lax.rem(self.z + dz, 4) * 4 + lax.rem(self.x + dx, 4)) * 2 + self.c
+
+    def back1(self, k, d):
+        ref = self.own(0, 0, k)
+        to = self.chip_at(0, d) if k else self.chip_at(d, 0)
+        return remote(ref, ref, self.wide_send.at[k, 4, d], self.wide_recv.at[k, 4, d], to, self.s)
+
+    def back2(self, k, i, d):
+        ref = self.own(0, i, k) if k else self.own(i, 0, k)
+        to = self.chip_at(d, 0) if k else self.chip_at(0, d)
+        return remote(ref, ref, self.wide_send.at[k, i, d], self.wide_recv.at[k, i, d], to, self.s)
 
     def join(self, t):
         ref = self.sum_s.at[pl.ds(self.base + self.c * self.half + self.line(t), 4 * self.piece)]
@@ -307,15 +315,29 @@
         total = self.b3[0].astype(F32)
         for j in range(1, 4):
             total = total + self.b3[j].astype(F32)
-        self.own(self.chip)[...] = total.astype(BF16)
-        for t in (2, 1, 3, 0):
-            for to in self.chips(t):
-                self.back(to).start()
+        at = self.base + self.c * self.half + self.chip * self.piece
+        self.sum_s[pl.ds(at, self.piece)] = total.astype(BF16)
+        for k in range(2):
+            for d in (2, 1, 3):
+                self.back1(k, d).start()
+        for k in range(2):
+            for d in (2, 1, 3):
+                self.back2(k, 0, d).start()
+
+    def step3b(self):
+        for i in (1, 3, 2):
+            for k in range(2):
+                self.back1(k, 4 - i).wait_recv()
+                for d in (2, 1, 3):
+                    self.back2(k, i, d).start()
 
     def step4(self):
         for t in (0, 1, 3, 2):
-            for frm in self.chips(t):
-                self.back_from(frm).wait_recv()
+            for d in range(1, 4):
+                self.back2(0, t, d).wait_recv()
+            if t:
+                for i in range(4):
+                    self.back2(1, i, 4 - t).wait_recv()
             self.join(t).start()
 
     def step5(self):
@@ -328,12 +350,18 @@
             self.join(t).wait_send()
             for to in self.chips(t):
                 self.spread(to).wait_send()
-                self.back(to).wait_send()
         for d in range(1, 4):
             self.gather3(d).wait_send()
-
-
-PARTS = (256, 192, 192)
+            for k in range(2):
+                self.back1(k, d).wait_send()
+                for i in range(4):
+                    self.back2(k, i, d).wait_send()
+
+
+PARTS = (256, 256, 128)
+BLOCKS = ([(0, i) for i in range(4)] + [(1, i) for i in range(4)]
+          + [(0, 4 * part + i) for part in (1, 2, 3) for i in (0, 1)]
+          + [(0, 4 * part + 2) for part in (1, 2, 3)] + [(0, 4 * part + 3) for part in (1, 2, 3)])
 
 
 def whole(n_emb, n_seq, len_ref, asked_ref, ev_ref, table_ref, win_ref, wout_ref, og_ref,
@@ -341,6 +369,7 @@
           idx_ref, tgb_s, req_ref, table_v, rows_v, tab_s, win_s, wout_s, og_s, lo_s, g_s, sum_s, sg_s, all_s,
           bufs_e, bufs_m, bufs_l, load, save, i_send, i_recv, j_send, j_recv, r_send, r_recv, g_send, g_recv,
           y_send, y_recv, z_send, z_recv, many_send, many_recv, few_send, few_recv,
+          wide_send, wide_recv,
           events_s, pick_s, normed_s, normed_t, rstd_s, gate_s, dsil_s, qkv_s, kv_t,
           att_t, p_s, d_s, gated_t, dx_s, do_s, dq_t, eg_s):
     e, s = lax.axis_index("emb"), lax.axis_index("seq")
@@ -368,14 +397,16 @@
     def asked(frm):
         return remote(req_ref.at[frm], idx_ref.at[s, frm], i_send.at[frm], i_recv.at[frm], frm, s)
 
-    rows_asked = asked_ref[0, 0]
+    rows_asked = asked_ref[...]
+    first = (((0,), (0,)), ((), ()))
     spot = jnp.where(lax.broadcasted_iota(jnp.int32, (cap, 128), 1)
                      == lax.broadcasted_iota(jnp.int32, (cap, 128), 0) + cap * inner, 1.0, 0.0)
     low = rows_asked & 127
     high = (rows_asked - low).astype(F32)
-    spread_out = (jnp.dot(high.astype(BF16), spot.astype(BF16), preferred_element_type=F32)
-                  + jnp.dot(low.astype(F32).astype(BF16), spot.astype(BF16),
-                            preferred_element_type=F32)).astype(jnp.int32)
+    spot = spot.astype(BF16)
+    spread_out = (lax.dot_general(high.astype(BF16), spot, first, preferred_element_type=F32)
+                  + lax.dot_general(low.astype(F32).astype(BF16), spot, first,
+                                    preferred_element_type=F32)).astype(jnp.int32)
     for to in range(n_emb):
         req_ref[to] = spread_out[to : to + 1, :]
     for j in (2, 1, 3, 0):
@@ -393,11 +424,18 @@
         return remote(rows_v.at[j, rows_of(lax.rem(frm, per), cap)], tab_s.at[rows_of(frm, cap)],
                       r_send.at[frm], r_recv.at[frm], frm, s)
 
+    def tell(d):
+        to = lax.rem(s + d, n_seq)
+        return remote(idx_ref.at[s], idx_ref.at[s], j_send.at[d], j_recv.at[d], e, to)
+
     loads[0].wait()
     for j in (0, 1, 3, 2):
         g, them = members(j)
         for frm in them:
             asked(frm).wait_recv()
+        if j == 2:
+            for d in range(1, n_seq):
+                tell(d).start()
         row = idx_ref[s, g * per]
         for i in range(1, per):
             row = row + idx_ref[s, g * per + i]
@@ -409,12 +447,18 @@
         if j == 0:
             tab_s[rows_of(e, cap), :] = rows_v[0, rows_of(inner, cap), :]
 
-    def tell(d):
-        to = lax.rem(s + d, n_seq)
-        return remote(idx_ref.at[s], idx_ref.at[s], j_send.at[d], j_recv.at[d], e, to)
-
-    for d in range(1, n_seq):
-        tell(d).start()
+    part = shard // n_seq
+    sub = lax.broadcasted_iota(jnp.int32, (part, 128), 0) + s * part
+    for n in range(n_seq):
+        if n:
+            tell(n).wait_recv()
+        frm = lax.rem(s + 2 * n_seq - n, n_seq)
+        for g in range(groups):
+            row = idx_ref[frm, g * per]
+            for i in range(1, per):
+                row = row + idx_ref[frm, g * per + i]
+            table_v[n * part : (n + 1) * part, g * 128 : (g + 1) * 128] = jnp.where(
+                sub == row, 1.0, 0.0).astype(BF16)
     for j in range(groups):
         for frm in members(j)[1]:
             answered(frm, j).wait_recv()
@@ -442,7 +486,8 @@
                                 preferred_element_type=F32))
     sums, base = [], 0
     for i, (units, bufs) in enumerate(zip(PARTS, (bufs_e, bufs_m, bufs_l))):
-        sems = [sem.at[i] for sem in (many_send, many_recv, few_send, few_recv)]
+        sems = [sem.at[i] for sem in (
+            many_send, many_recv, few_send, few_recv, wide_send, wide_recv)]
         sums.append(Summed(e, s, base, units, g_s, sum_s, bufs, sems))
         base += units
     early, mid, late = sums
@@ -451,23 +496,25 @@
     def back(h):
         attend_back(h, qkv_s, kv_t, p_s, d_s, do_s, dsil_s, dx_s, dq_t, blocks, width)
 
-    def grads_of(c):
-        for b in range(3):
-            cols = slice((b + 1) * width + c * B, (b + 1) * width + (c + 1) * B)
-            put_grad(4 + 3 * c + b, jnp.dot(normed_t[...], dx_s[:, cols],
-                                            preferred_element_type=F32))
+    def grads_of(first, last):
+        for b in range(first, last, 2):
+            pair = [BLOCKS[i][1] * 128 for i in range(b, min(b + 2, last))]
+            cols = jnp.concatenate([dx_s[:, at : at + 128] for at in pair], axis=1)
+            val = jnp.dot(normed_t[...], cols, preferred_element_type=F32).astype(BF16)
+            for i in range(len(pair)):
+                g_s[(b + i) * 32 : (b + i + 1) * 32] = (
+                    val[:, i * 128 : (i + 1) * 128].reshape(32, 16, 128))
 
     back(0)
     early.step1()
     back(1)
-    grads_of(0)
+    back(2)
+    grads_of(8, 16)
     mid.step0()
-    back(2)
-    mid.step1()
     back(3)
     early.step2()
+    mid.step1()
     pl.loop(0, blocks)(lambda r: event_back(r, dx_s, win_s, normed_s, rstd_s, og_s, eg_s))
-    early.step3()
     sg_s[...] = jnp.dot(pick_s[...], eg_s[...], preferred_element_type=F32).astype(BF16)
 
     def give(to):
@@ -482,9 +529,9 @@
         for to in members(j)[1]:
             give(to).start()
     all_s[s, rows_of(e, cap), :] = sg_s[rows_of(e, cap), :]
-    grads_of(1)
+    early.step3()
+    grads_of(16, 20)
     late.step0()
-    mid.step2()
     chunk = all_s.shape[1] // groups
     up, down = lax.rem(s + 1, n_seq), lax.rem(s + n_seq - 1, n_seq)
 
@@ -507,86 +554,58 @@
         pass_on(j, 0 if j % 2 else 1).wait_recv()
         relay(j).start()
 
+    def add(n):
+        frm = lax.rem(s + 2 * n_seq - n, n_seq)
+
+        @pl.loop(0, blocks)
+        def _(r):
+            at = pl.ds(pl.multiple_of(n * part + r * B, B), B)
+            val = jnp.dot(table_v[at, :], all_s[frm], preferred_element_type=F32)
+            if n == 0:
+                gate_s[rows_at(r), :] = val
+            elif n == 2:
+                tgb_s[rows_at(r), :] = (gate_s[rows_at(r), :] + val).astype(BF16)
+            else:
+                gate_s[rows_at(r), :] += val
+
     def keep(i):
         rows = pl.ds(sums[i].base, PARTS[i])
         saves.append(pltpu.make_async_copy(sum_s.at[rows], total_ref.at[rows], save.at[2 + i]))
         saves[-1].start()
 
-    part = gate_s.shape[0]
-    sub = lax.broadcasted_iota(jnp.int32, (part, 128), 0) + s * part
-    for d in range(1, n_seq):
-        tell(d).wait_recv()
-    for n in range(n_seq):
-        for j in range(groups):
-            g = lax.rem(mine + j, groups)
-            frm = lax.rem(s + n, n_seq)
-            row = idx_ref[frm, g * per]
-            for i in range(1, per):
-                row = row + idx_ref[frm, g * per + i]
-            at = (n * groups + j) * 128
-            dsil_s[:, at : at + 128] = jnp.where(sub == row, 1.0, 0.0).astype(BF16)
-
-    def add(n, js):
-        frm = lax.rem(s + n, n_seq)
-        rows = jnp.concatenate(
-            [all_s[frm, rows_of(lax.rem(mine + j, groups), chunk), :] for j in js], axis=0)
-        at = (n * groups + js[0]) * 128
-
-        @pl.loop(0, blocks)
-        def _(r):
-            val = jnp.dot(dsil_s[rows_at(r), at : at + 256], rows, preferred_element_type=F32)
-            if n == 0 and js[0] == 0:
-                gate_s[rows_at(r), :] = val
-            else:
-                gate_s[rows_at(r), :] += val
-
-    def keep(i):
-        rows = pl.ds(sums[i].base, PARTS[i])
-        saves.append(pltpu.make_async_copy(sum_s.at[rows], total_ref.at[rows], save.at[2 + i]))
-        saves[-1].start()
-
     arrived(0)
     late.step1()
+    early.step3b()
+    mid.step2()
     arrived(1)
+    further(0)
+    late.step2()
+    arrived(2)
+    early.step4()
     mid.step3()
-    early.step4()
-    further(0)
-    add(0, (0, 1))
-    arrived(2)
-    late.step2()
     further(1)
+    late.step3()
     arrived(3)
-    mid.step4()
-    add(0, (2, 3))
-    late.step3()
+    mid.step3b()
     further(2)
+    late.step3b()
+    add(0)
     early.step5()
     keep(0)
-    for way in range(2):
-        for j in (0, 1):
-            if way != (0 if j % 2 else 1):
-                pass_on(j, way).wait_recv()
-    add(1, (0, 1))
-    add(3, (0, 1))
     further(3)
+    mid.step4()
+    late.step4()
+    for j in range(groups):
+        pass_on(j, 1 if j % 2 else 0).wait_recv()
+    add(1)
+    add(3)
     mid.step5()
     keep(1)
-    late.step4()
-    for way in range(2):
-        for j in (2, 3):
-            if way != (0 if j % 2 else 1):
-                pass_on(j, way).wait_recv()
-    add(1, (2, 3))
-    add(3, (2, 3))
-    relay(0).wait_recv()
-    relay(1).wait_recv()
-    add(2, (0, 1))
     late.step5()
     keep(2)
-    relay(2).wait_recv()
-    relay(3).wait_recv()
-    add(2, (2, 3))
-    tgb_s[...] = gate_s[...].astype(BF16)
+    for j in range(groups):
+        relay(j).wait_recv()
+    add(2)
     saves.append(pltpu.make_async_copy(tgb_s, tg_ref, save.at[1]))
     saves[-1].start()
     for d in range(1, n_seq):
@@ -648,6 +667,7 @@
             dma((n_emb,)), dma((n_emb,)), dma((n_emb,)), dma((n_emb,)),
             dma((2, 4)), dma((2, 4)), dma((4,)), dma((4,)),
             dma((3, 2, 16)), dma((3, 2, 16)), dma((3, 3, 4)), dma((3, 3, 4)),
+            dma((3, 2, 5, 4)), dma((3, 2, 5, 4)),
         ] + compute_scratch(tokens, width, slots),
         compiler_params=pltpu.CompilerParams(
             collective_id=0, has_side_effects=True, vmem_limit_bytes=67043328),
@@ -671,12 +691,8 @@
         for b in range(20):
             val = sum_s[b * 32 + r * 8 : b * 32 + r * 8 + 8].reshape(tall, 128).astype(F32)
             rows = slice(r * tall, (r + 1) * tall)
-            if 4 <= b < 8:
-                wo_v[rows, (b - 4) * 128 : (b - 3) * 128] = val
-            else:
-                half, part, head = (b - 8) // 6, (b - 8) % 6 // 2, b % 2
-                at = b if b < 4 else 4 + part * 4 + half * 2 + head
-                wi_v[rows, at * 128 : (at + 1) * 128] = val
+            which, at = BLOCKS[b]
+            (wo_v if which else wi_v)[rows, at * 128 : (at + 1) * 128] = val
         copies.append(pltpu.make_async_copy(wi_v.at[rows], wi_ref.at[rows], sems.at[r]))
         copies[-1].start()
     copies.append(pltpu.make_async_copy(wo_v, wo_ref, sems.at[4]))
@@ -709,7 +725,7 @@
     n_emb, n_seq = lax.axis_size("emb"), lax.axis_size("seq")
     cap = fetch_rows.shape[-1]
     layer_out, rows_grad, total = layer_grads(
-        lengths, fetch_rows, event_slot.reshape(-1, 128), item_table,
+        lengths, jnp.swapaxes(fetch_rows, 2, 3).reshape(cap, n_emb), event_slot.reshape(-1, 128), item_table,
         in_weight, out_weight, out_grad, n_emb, n_seq, n_emb * cap)
     table_grad, in_total, out_total, layer_out = finish_grads(rows_grad, total, layer_out)
     return layer_out, table_grad, in_total, out_total

time: 107 us -> 104 us (0.972)
  Pallas kernels: 104 us -> 101 us
  local copies, waits for them, and re-layouts: 1.38 us -> 0 us
    pallas_call x1, Pallas kernels: 98.8 us -> 96.2 us  [layer_grads(): pl.pallas_call(functools.partial(whole, n_emb, n_seq), name='layer', out_...]
    unnamed x1 -> x0, local copies, waits for them, and re-layouts: 1.38 us -> none
where the time goes in v3:
time: 104 us; the launch traced here: 102 us
  Pallas kernels  101 us (97%)
    pallas_call x1, Pallas kernels, layer_grads(): pl.pallas_call(functools.partial(whole, n_emb, n_seq), name='layer', out_...  96.2 us
    pallas_call x1, Pallas kernels, finish_grads(): pl.pallas_call(finish, name='finish', out_shape=tuple((jax.ShapeDtypeStru...  4.87 us

profile of v3, /device:TPU:1, one launch (start us, length us, event | category | flops | bytes accessed | tf_op | source)
XLA Modules:
  0.0 101.9 jit_solution(9978385051832852784)
XLA Ops:
  0.6 96.2 %layer.1 = (bf16[1024,512]{1,0:T(8,128)(2,1)}, bf16[1024,512]{1,0:T(8,128)(2,1)}, bf16[640,16,128]{2,1,0:T(8,128)(2,1)}) custom-call(s32[1,8]{1,0:T(1,128)} %len_ref.1, s32[16,32]{1,0:T(8,128)} %bitcast.4, s32[8,128]{1,0:T(8,128)} %bitcast.5, bf16[4096,512]{1,0:T(8,128)(2,1)} %table_ref.1, bf16[512,2048]{1,0:T(8,128)(2,1)} %win_ref.1, ...), custom_call_target="tpu_custom_call" | custom-call | tf_op jit(solution)/shard_map/layer/pallas_call | solution.py:639
  96.9 4.9 %finish.1 = (f32[1024,512]{1,0:T(8,128)}, f32[512,2048]{1,0:T(8,128)}, f32[512,512]{1,0:T(8,128)}, bf16[1024,512]{1,0:T(8,128)(2,1)}) custom-call(bf16[1024,512]{1,0:T(8,128)(2,1)} %get-tuple-element.11.rows_ref, bf16[640,16,128]{2,1,0:T(8,128)(2,1)} %get-tuple-element.12.sum_ref, bf16[1024,512]{1,0:T(8,128)(2,1)} %get-tuple-element.13.out_ref), custom_call_target="tpu_custom_call" | custom-call | tf_op jit(solution)/shard_map/finish/pallas_call | solution.py:711

commit v4 on v3

--- a/solution.py
+++ b/solution.py
@@ -512,9 +512,13 @@
     grads_of(8, 16)
     mid.step0()
     back(3)
+    grads_of(16, 20)
+    late.step0()
     early.step2()
     mid.step1()
     pl.loop(0, blocks)(lambda r: event_back(r, dx_s, win_s, normed_s, rstd_s, og_s, eg_s))
+    early.step3()
+    late.step1()
     sg_s[...] = jnp.dot(pick_s[...], eg_s[...], preferred_element_type=F32).astype(BF16)
 
     def give(to):
@@ -529,9 +533,6 @@
         for to in members(j)[1]:
             give(to).start()
     all_s[s, rows_of(e, cap), :] = sg_s[rows_of(e, cap), :]
-    early.step3()
-    grads_of(16, 20)
-    late.step0()
     chunk = all_s.shape[1] // groups
     up, down = lax.rem(s + 1, n_seq), lax.rem(s + n_seq - 1, n_seq)
 
@@ -573,28 +574,27 @@
         saves.append(pltpu.make_async_copy(sum_s.at[rows], total_ref.at[rows], save.at[2 + i]))
         saves[-1].start()
 
+    mid.step2()
+    early.step3b()
     arrived(0)
-    late.step1()
-    early.step3b()
-    mid.step2()
+    late.step2()
     arrived(1)
+    mid.step3()
     further(0)
-    late.step2()
+    early.step4()
     arrived(2)
-    early.step4()
-    mid.step3()
+    late.step3()
+    mid.step3b()
     further(1)
-    late.step3()
     arrived(3)
-    mid.step3b()
-    further(2)
-    late.step3b()
-    add(0)
     early.step5()
     keep(0)
+    late.step3b()
+    mid.step4()
+    further(2)
+    add(0)
+    late.step4()
     further(3)
-    mid.step4()
-    late.step4()
     for j in range(groups):
         pass_on(j, 1 if j % 2 else 0).wait_recv()
     add(1)

time: 104 us -> 104 us (level); the launches traced: 102 us -> 104 us
  Pallas kernels: 101 us -> 103 us
    pallas_call x1, Pallas kernels: 96.2 us -> 98.1 us  [layer_grads(): pl.pallas_call(functools.partial(whole, n_emb, n_seq), name='layer', out_...]
where the time goes in v4:
time: 104 us
  Pallas kernels  103 us (99%)
    pallas_call x1, Pallas kernels, layer_grads(): pl.pallas_call(functools.partial(whole, n_emb, n_seq), name='layer', out_...  98.1 us
    pallas_call x1, Pallas kernels, finish_grads(): pl.pallas_call(finish, name='finish', out_shape=tuple((jax.ShapeDtypeStru...  4.87 us

profile of v4, /device:TPU:1, one launch (start us, length us, event | category | flops | bytes accessed | tf_op | source)
XLA Modules:
  0.0 103.7 jit_solution(14091236782152511361)
XLA Ops:
  0.6 98.1 %layer.1 = (bf16[1024,512]{1,0:T(8,128)(2,1)}, bf16[1024,512]{1,0:T(8,128)(2,1)}, bf16[640,16,128]{2,1,0:T(8,128)(2,1)}) custom-call(s32[1,8]{1,0:T(1,128)} %len_ref.1, s32[16,32]{1,0:T(8,128)} %bitcast.4, s32[8,128]{1,0:T(8,128)} %bitcast.5, bf16[4096,512]{1,0:T(8,128)(2,1)} %table_ref.1, bf16[512,2048]{1,0:T(8,128)(2,1)} %win_ref.1, ...), custom_call_target="tpu_custom_call" | custom-call | tf_op jit(solution)/shard_map/layer/pallas_call | solution.py:639
  98.7 4.9 %finish.1 = (f32[1024,512]{1,0:T(8,128)}, f32[512,2048]{1,0:T(8,128)}, f32[512,512]{1,0:T(8,128)}, bf16[1024,512]{1,0:T(8,128)(2,1)}) custom-call(bf16[1024,512]{1,0:T(8,128)(2,1)} %get-tuple-element.11.rows_ref, bf16[640,16,128]{2,1,0:T(8,128)(2,1)} %get-tuple-element.12.sum_ref, bf16[1024,512]{1,0:T(8,128)(2,1)} %get-tuple-element.13.out_ref), custom_call_target="tpu_custom_call" | custom-call | tf_op jit(solution)/shard_map/finish/pallas_call | solution.py:711
